TPU v7x, 32 devices: a whole 2x2x4 slice. The times are simulated.
32 devices in a mesh: seq: 8 (over y, x, core), rep: 4 (over z).
Axes of the slice: x: 2, y: 2, z: 4, core: 2. Of those that a mesh axis runs over, the one named last changes fastest.
Arguments:
- query_rows: bfloat16 [8, 8, 256, 1152], P('rep', 'seq'), as said below
- key_rows: bfloat16 [8, 8, 256, 1152], P('rep', 'seq'), as said below
- value_rows: bfloat16 [8, 8, 256, 1152], P('rep', 'seq'), may hold values from -6 to 6
- out_grad: bfloat16 [8, 8, 256, 1152], P('rep', 'seq'), may hold values from -6 to 6
- out_weight: bfloat16 [1152, 1152], replicated, may hold values from -0.1875 to 0.1875
- frame_count: int32 [8], P('rep'), may hold values from 1 to 8, as said below
- pos_count: int32 [8], P('rep'), may hold values from 64 to 256, as said below
Outputs:
- projected: bfloat16 [8, 8, 256, 1152], P('rep', 'seq')
- grad_query: bfloat16 [8, 8, 256, 1152], P('rep', 'seq')
- grad_key: bfloat16 [8, 8, 256, 1152], P('rep', 'seq')
- grad_value: bfloat16 [8, 8, 256, 1152], P('rep', 'seq')
- grad_weight: float32 [1152, 1152], P('seq')
Inputs may be any that keep to these rules, and one draw needn't show every extreme that they name: `query_rows`: entries lie within -40 to 40. `key_rows`: entries lie within -40 to 40. `frame_count`: some clip has all 8 frames live. `pos_count`: some clip has all 256 positions live.
All inputs are finite; a program needn't handle non-finite values.
Results may differ from a plain program's by a relative error of at most 0.0057.
Values may be sent and summed in bfloat16 or wider, within the bound.
No kernel may reach another device: no remote copies, remote signals or barrier semaphores. Data moves between devices by JAX's collectives and lax.ppermute only.
A program may use at most 128 MiB of HBM per device.

v0:
```python
import math

import jax
import jax.numpy as jnp
from jax import lax
from jax.sharding import PartitionSpec as P

HEADS = 16


def attend_local(query_part, key_part, value_part, key_live, row_live):
    nframe, npos_part, width = query_part.shape
    head_dim = width // HEADS
    inv_root = 1.0 / math.sqrt(head_dim)
    shape_heads = (nframe, npos_part, HEADS, head_dim)
    query_heads = query_part.reshape(shape_heads)
    key_heads = key_part.reshape(shape_heads)
    value_heads = value_part.reshape(shape_heads)
    scores = (
        jnp.einsum("fphd,tphd->phft", query_heads, key_heads, preferred_element_type=jnp.float32)
        * inv_root
    )
    scores = jnp.where(key_live, scores, -1e30)
    highest = jnp.max(scores, axis=-1, keepdims=True)
    expo = jnp.exp(scores - highest) * key_live.astype(jnp.float32)
    weights = expo / jnp.sum(expo, axis=-1, keepdims=True)
    rounded = weights.astype(jnp.bfloat16)
    mixed = jnp.einsum("phft,tphd->fphd", rounded, value_heads, preferred_element_type=jnp.float32)
    attn_out = jnp.where(row_live[:, :, None], mixed.reshape(nframe, npos_part, width), 0.0).astype(
        jnp.bfloat16
    )
    return (attn_out, weights, rounded)


def attend_back(query_part, key_part, value_part, cot_part, weights, rounded):
    nframe, npos_part, width = query_part.shape
    head_dim = width // HEADS
    inv_root = 1.0 / math.sqrt(head_dim)
    shape_heads = (nframe, npos_part, HEADS, head_dim)
    cot_heads = cot_part.reshape(shape_heads)
    value_heads = value_part.reshape(shape_heads)
    grad_value = jnp.einsum(
        "phft,fphd->tphd", rounded, cot_heads, preferred_element_type=jnp.float32
    )
    grad_attn = jnp.einsum(
        "fphd,tphd->phft", cot_heads, value_heads, preferred_element_type=jnp.float32
    )
    row_delta = jnp.sum(weights * grad_attn, axis=-1, keepdims=True)
    grad_score = weights * (grad_attn - row_delta) * inv_root
    key_wide = key_part.astype(jnp.float32).reshape(shape_heads)
    query_wide = query_part.astype(jnp.float32).reshape(shape_heads)
    grad_query = jnp.einsum(
        "phft,tphd->fphd", grad_score, key_wide, precision=lax.Precision.HIGHEST
    )
    grad_key = jnp.einsum(
        "phft,fphd->tphd", grad_score, query_wide, precision=lax.Precision.HIGHEST
    )
    full = (nframe, npos_part, width)
    return (
        grad_query.reshape(full).astype(jnp.bfloat16),
        grad_key.reshape(full).astype(jnp.bfloat16),
        grad_value.reshape(full).astype(jnp.bfloat16),
    )


def reduce_weight(flat_grad, flat_out):
    mine = lax.psum_scatter(
        lax.dot_general(
            flat_grad, flat_out, (((0,), (0,)), ((), ())), preferred_element_type=jnp.float32
        ),
        "seq",
        scatter_dimension=0,
        tiled=True,
    )
    return lax.psum(mine, "rep")


def shards(query_rows, key_rows, value_rows, out_grad, out_weight, frame_count, pos_count):
    clip_local, frame_local, npos_all, width = query_rows.shape
    rank = lax.axis_index("seq")
    query_pos, key_pos, value_pos = (
        lax.all_to_all(query_rows, "seq", split_axis=2, concat_axis=1, tiled=True),
        lax.all_to_all(key_rows, "seq", split_axis=2, concat_axis=1, tiled=True),
        lax.all_to_all(value_rows, "seq", split_axis=2, concat_axis=1, tiled=True),
    )
    nframe = query_pos.shape[1]
    npos_part = query_pos.shape[2]
    frame_ids = jnp.arange(nframe, dtype=jnp.int32)
    position_ids = rank * npos_part + jnp.arange(npos_part, dtype=jnp.int32)
    key_live = frame_ids[None, :] < frame_count[:, None]
    row_live = key_live[:, :, None] & (position_ids[None, None, :] < pos_count[:, None, None])
    attn_pos, weights, rounded = jax.vmap(attend_local)(
        query_pos, key_pos, value_pos, key_live, row_live
    )
    attn_frames = lax.all_to_all(attn_pos, "seq", split_axis=1, concat_axis=2, tiled=True)
    flat_out = attn_frames.reshape(-1, width)
    flat_grad = out_grad.reshape(-1, width)
    projected = lax.dot_general(
        flat_out, out_weight, (((1,), (1,)), ((), ())), preferred_element_type=jnp.float32
    )
    projected = projected.astype(jnp.bfloat16).reshape(query_rows.shape)
    own_frames = rank * frame_local + jnp.arange(frame_local, dtype=jnp.int32)
    frame_alive = own_frames[None, :, None] < frame_count[:, None, None]
    place_alive = jnp.arange(npos_all, dtype=jnp.int32)[None, None, :] < pos_count[:, None, None]
    out_cot = jnp.dot(flat_grad, out_weight, preferred_element_type=jnp.float32).reshape(
        query_rows.shape
    )
    out_cot = jnp.where((frame_alive & place_alive)[..., None], out_cot, 0.0).astype(jnp.bfloat16)
    cot_pos = lax.all_to_all(out_cot, "seq", split_axis=2, concat_axis=1, tiled=True)
    grad_query_pos, grad_key_pos, grad_value_pos = jax.vmap(attend_back)(
        query_pos, key_pos, value_pos, cot_pos, weights, rounded
    )
    grad_query, grad_key, grad_value = (
        lax.all_to_all(grad_query_pos, "seq", split_axis=1, concat_axis=2, tiled=True),
        lax.all_to_all(grad_key_pos, "seq", split_axis=1, concat_axis=2, tiled=True),
        lax.all_to_all(grad_value_pos, "seq", split_axis=1, concat_axis=2, tiled=True),
    )
    grad_weight = reduce_weight(flat_grad, flat_out)
    return (projected, grad_query, grad_key, grad_value, grad_weight)


def solution(mesh):
    in_specs = (
        P("rep", "seq", None, None),
        P("rep", "seq", None, None),
        P("rep", "seq", None, None),
        P("rep", "seq", None, None),
        P(),
        P("rep"),
        P("rep"),
    )
    out_specs = (
        P("rep", "seq", None, None),
        P("rep", "seq", None, None),
        P("rep", "seq", None, None),
        P("rep", "seq", None, None),
        P("seq", None),
    )
    return jax.shard_map(shards, mesh=mesh, in_specs=in_specs, out_specs=out_specs, check_vma=False)
```

profile of v0, /device:TPU:0, one launch (start us, length us, event | category | flops | bytes accessed | tf_op | source)
XLA Modules:
  0.0 297.7 jit_solution(12987899901119479207)
XLA Ops:
  7.2 0.0 copy-start
  7.2 3.6 %copy.97 = bf16[2,1,256,1152]{3,0,1,2:T(2,128)(2,1)} copy(bf16[2,1,256,1152]{3,2,1,0:T(8,128)(2,1)} %param.7) | data formatting | bytes 2359296 | tf_op args[0]
  10.8 5.2 %all-to-all-start = ((bf16[2,1,256,1152]{3,0,1,2:T(2,128)(2,1)}), bf16[2,1,256,1152]{3,0,1,2:T(2,128)(2,1)}, u32[]{:S(2)}, u32[]{:S(2)}) async-start(bf16[2,1,256,1152]{3,0,1,2:T(2,128)(2,1)} %copy.97), calls=%async_computation | async-start | bytes 2359296 | tf_op jit(solution)/shard_map/all_to_all | solution.py:82
  16.0 3.5 %copy.99 = bf16[2,1,256,1152]{3,0,1,2:T(2,128)(2,1)} copy(bf16[2,1,256,1152]{3,2,1,0:T(8,128)(2,1)} %param.8) | data formatting | bytes 2359296 | tf_op args[1]
  19.5 13.4 %all-to-all-done = bf16[2,1,256,1152]{3,0,1,2:T(2,128)(2,1)} async-done(((bf16[2,1,256,1152]{3,0,1,2:T(2,128)(2,1)}), bf16[2,1,256,1152]{3,0,1,2:T(2,128)(2,1)}, u32[]{:S(2)}, u32[]{:S(2)}) %all-to-all-start) | async-done | bytes 1179680 | tf_op jit(solution)/shard_map/all_to_all | solution.py:82
  32.9 4.3 %all-to-all-start.1 = ((bf16[2,1,256,1152]{3,0,1,2:T(2,128)(2,1)}), bf16[2,1,256,1152]{3,0,1,2:T(2,128)(2,1)}, u32[]{:S(2)}, u32[]{:S(2)}) async-start(bf16[2,1,256,1152]{3,0,1,2:T(2,128)(2,1)} %copy.99), calls=%async_computation.1 | async-start | bytes 2359296 | tf_op jit(solution)/shard_map/all_to_all | solution.py:83
  37.2 0.0 copy-start.6
  37.2 0.0 copy-start.5
  37.2 3.5 %copy.103 = bf16[2,1,256,1152]{3,0,1,2:T(2,128)(2,1)} copy(bf16[2,1,256,1152]{3,2,1,0:T(8,128)(2,1)} %param.9) | data formatting | bytes 2359296 | tf_op args[2]
  40.7 13.3 %all-to-all-done.1 = bf16[2,1,256,1152]{3,0,1,2:T(2,128)(2,1)} async-done(((bf16[2,1,256,1152]{3,0,1,2:T(2,128)(2,1)}), bf16[2,1,256,1152]{3,0,1,2:T(2,128)(2,1)}, u32[]{:S(2)}, u32[]{:S(2)}) %all-to-all-start.1) | async-done | bytes 1179680 | tf_op jit(solution)/shard_map/all_to_all | solution.py:83
  54.0 4.2 %all-to-all-start.2 = ((bf16[2,1,256,1152]{3,0,1,2:T(2,128)(2,1)}), bf16[2,1,256,1152]{3,0,1,2:T(2,128)(2,1)}, u32[]{:S(2)}, u32[]{:S(2)}) async-start(bf16[2,1,256,1152]{3,0,1,2:T(2,128)(2,1)} %copy.103), calls=%async_computation.2 | async-start | bytes 2359296 | tf_op jit(solution)/shard_map/all_to_all | solution.py:84
  58.2 0.2 reduce-scatter.4.cloned.1.call-start
  58.5 0.1 broadcast_compare_fusion
  58.5 0.1 iota_compare_fusion
  58.6 0.1 broadcast_and_fusion
  58.7 6.5 %reshape.214 = bf16[2,8,32,16,72]{4,3,0,2,1:T(8,128)(2,1)} reshape(bf16[2,1,256,1152]{3,0,1,2:T(2,128)(2,1)} %all-to-all-done) | data formatting | bytes 2359296 | tf_op jit(solution)/shard_map/vmap()/reshape | solution.py:16
  65.2 6.5 %reshape.215 = bf16[2,8,32,16,72]{4,3,0,2,1:T(8,128)(2,1)} reshape(bf16[2,1,256,1152]{3,0,1,2:T(2,128)(2,1)} %all-to-all-done.1) | data formatting | bytes 2359296 | tf_op jit(solution)/shard_map/vmap()/reshape | solution.py:17
  71.7 8.7 %fusion.38 = (f32[2,32,16,8]{3,2,1,0:T(8,128)S(1)}, f32[2,32,16,8,8]{3,4,2,1,0:T(8,128)}) fusion(f32[2,8]{1,0:T(2,128)S(1)} %get-tuple-element.31, pred[2,8]{1,0:T(4,128)(4,1)S(1)} %get-tuple-element.30, bf16[2,8,32,16,72]{4,3,0,2,1:T(8,128)(2,1)} %reshape.215, bf16[2,8,32,16,72]{4,3,0,2,1:T(8,128)(2,1)} %reshape.214), kind=kOutput, calls=%fused_computation.48 | convolution fusion | flops 9764871 | bytes 2654288 | tf_op jit(solution)/shard_map/vmap()/sub | solution.py:25
  80.4 0.0 all-to-all-done.2
  80.4 6.5 %reshape.216 = bf16[2,8,32,16,72]{4,3,0,2,1:T(8,128)(2,1)} reshape(bf16[2,1,256,1152]{3,0,1,2:T(2,128)(2,1)} %all-to-all-done.2) | data formatting | bytes 2359296 | tf_op jit(solution)/shard_map/vmap()/reshape | solution.py:18
  87.0 4.1 %convolution_bitcast_fusion.1 = bf16[2,8,32,16,72]{4,1,3,2,0:T(8,128)(2,1)S(1)} fusion(bf16[2,8,32,16,72]{4,3,0,2,1:T(8,128)(2,1)} %reshape.216, f32[2,32,16,8,8]{3,4,2,1,0:T(8,128)} %get-tuple-element.33, f32[2,32,16,8]{3,2,1,0:T(8,128)S(1)} %get-tuple-element.32), kind=kOutput, calls=%fused_computation.13 | convolution fusion | flops 9568256 | bytes 2654208 | tf_op jit(solution)/shard_map/vmap(phft,tphd->fphd)/dot_general | solution.py:28
  91.0 1.7 copy.107
  92.8 4.6 %reshape.203 = bf16[2,8,32,1152]{3,2,1,0:T(8,128)(2,1)} reshape(bf16[2,8,32,16,72]{4,3,2,1,0:T(8,128)(2,1)} %copy.107) | data formatting | bytes 2359296 | tf_op jit(solution)/shard_map/vmap()/reshape | solution.py:29
  97.3 1.5 select_convert_fusion
  98.9 0.1 copy.108
  99.0 0.0 copy-start.4
  99.0 20.7 %all_to_all.81 = bf16[2,8,32,1152]{3,2,0,1:T(8,128)(2,1)S(1)} all-to-all(bf16[2,8,32,1152]{3,2,0,1:T(8,128)(2,1)S(1)} %copy.108), channel_id=1, replica_groups=mesh['seq'=8,'rep'=4] {'seq'}, dimensions={1} | all-to-all | bytes 2359296 | tf_op jit(solution)/shard_map/all_to_all | solution.py:95
  119.8 0.1 copy.109
  119.9 0.0 copy-start.1
  119.9 1.0 copy-done.1
  120.9 4.1 %convolution_bitcast_fusion = f32[1152,1152]{0,1:T(8,128)} fusion(bf16[512,1152]{1,0:T(8,128)(2,1)S(1)} %bitcast.59, bf16[512,1152]{1,0:T(8,128)(2,1)S(1)} %bitcast.64), kind=kOutput, calls=%fused_computation.1 | convolution fusion | flops 1358954496 | bytes 7667712 | tf_op jit(solution)/shard_map/dot_general | solution.py:68
  125.0 6.9 %copy.137 = f32[1152,1152]{1,0:T(8,128)} copy(f32[1152,1152]{0,1:T(8,128)} %convolution_bitcast_fusion) | data formatting | bytes 10616832
  131.9 0.0 reduce-scatter.4.cloned.1.call-update
  131.9 0.1 compare_and_fusion
  132.0 3.1 %fusion.3 = bf16[2,1,256,1152]{3,2,0,1:T(8,128)(2,1)S(1)} fusion(bf16[1152,1152]{1,0:T(8,128)(2,1)S(1)} %copy-done, bf16[2,1,256,1152]{3,2,1,0:T(8,128)(2,1)} %param.10, pred[2,256]{1,0:T(4,128)(4,1)S(1)} %compare_and_fusion), kind=kOutput, calls=%fused_computation.10 | convolution fusion | flops 1360134144 | bytes 5014016 | tf_op jit(solution)/shard_map/dot_general | solution.py:105
  135.1 1.2 copy.110
  136.3 19.9 %all_to_all.82 = bf16[2,1,256,1152]{3,0,1,2:T(2,128)(2,1)} all-to-all(bf16[2,1,256,1152]{3,0,1,2:T(2,128)(2,1)S(1)} %copy.110), channel_id=1, replica_groups=mesh['seq'=8,'rep'=4] {'seq'}, dimensions={2} | all-to-all | bytes 2359296 | tf_op jit(solution)/shard_map/all_to_all | solution.py:109
  156.2 6.5 %reshape.217 = bf16[2,8,32,16,72]{4,3,0,2,1:T(8,128)(2,1)} reshape(bf16[2,1,256,1152]{3,0,1,2:T(2,128)(2,1)} %all_to_all.82) | data formatting | bytes 2359296 | tf_op jit(solution)/shard_map/vmap()/reshape | solution.py:40
  162.7 4.7 %convert_bitcast_fusion = bf16[2,8,32,16,72]{4,1,3,2,0:T(8,128)(2,1)S(1)} fusion(bf16[2,8,32,16,72]{4,3,0,2,1:T(8,128)(2,1)} %reshape.217, f32[2,32,16,8,8]{3,4,2,1,0:T(8,128)} %get-tuple-element.33, f32[2,32,16,8]{3,2,1,0:T(8,128)S(1)} %get-tuple-element.32), kind=kOutput, calls=%fused_computation.14 | convolution fusion | flops 10158080 | bytes 2654208 | tf_op jit(solution)/shard_map/vmap(phft,fphd->tphd)/dot_general | solution.py:42
  167.4 1.8 copy.136
  169.2 4.6 %reshape.211 = bf16[2,8,32,1152]{3,2,0,1:T(8,128)(2,1)} reshape(bf16[2,8,32,16,72]{4,3,2,0,1:T(8,128)(2,1)} %copy.136) | data formatting | bytes 2359296 | tf_op jit(solution)/shard_map/vmap()/convert_element_type | solution.py:62
  173.8 4.7 %all-to-all-start.7 = ((bf16[2,8,32,1152]{3,2,0,1:T(8,128)(2,1)}), bf16[2,8,32,1152]{3,2,0,1:T(8,128)(2,1)}, u32[]{:S(2)}, u32[]{:S(2)}) async-start(bf16[2,8,32,1152]{3,2,0,1:T(8,128)(2,1)} %reshape.211), calls=%async_computation.7 | async-start | bytes 2359296 | tf_op jit(solution)/shard_map/all_to_all | solution.py:116
  178.5 9.1 %multiply_reduce_fusion = (f32[2,32,16,8]{3,2,1,0:T(8,128)S(1)}, f32[2,32,16,8,8]{3,4,2,1,0:T(8,128)}) fusion(f32[2,32,16,8,8]{3,4,2,1,0:T(8,128)} %get-tuple-element.33, f32[2,32,16,8]{3,2,1,0:T(8,128)S(1)} %get-tuple-element.32, bf16[2,8,32,16,72]{4,3,0,2,1:T(8,128)(2,1)} %reshape.216, bf16[2,8,32,16,72]{4,3,0,2,1:T(8,128)(2,1)} %reshape.217), kind=kOutput, calls=%fused_computation.3 | convolution fusion | flops 9625600 | bytes 2949120 | tf_op jit(solution)/shard_map/vmap(fphd,tphd->phft)/dot_general | solution.py:45
  187.6 7.4 %convert_bitcast_fusion.1 = bf16[2,8,32,16,72]{4,1,3,2,0:T(8,128)(2,1)S(1)} fusion(bf16[2,8,32,16,72]{4,3,0,2,1:T(8,128)(2,1)S(1)} %copy-done.3, f32[2,32,16,8,8]{3,4,2,1,0:T(8,128)} %get-tuple-element.35, f32[2,32,16,8]{3,2,1,0:T(8,128)S(1)} %get-tuple-element.34, f32[2,32,16,8,8]{3,4,2,1,0:T(8,128)S(1)} %copy-done.7, ...), kind=kOutput, calls=%fused_computation.15 | convolution fusion | flops 57475072 | bytes 2949120 | tf_op jit(solution)/shard_map/vmap(phft,fphd->tphd)/dot_general | solution.py:55
  195.0 1.9 copy.135
  196.9 4.6 %reshape.210 = bf16[2,8,32,1152]{3,2,0,1:T(8,128)(2,1)} reshape(bf16[2,8,32,16,72]{4,3,2,0,1:T(8,128)(2,1)} %copy.135) | data formatting | bytes 2359296 | tf_op jit(solution)/shard_map/vmap()/convert_element_type | solution.py:61
  201.4 0.0 all-to-all-done.7
  201.4 4.4 %all-to-all-start.6 = ((bf16[2,8,32,1152]{3,2,0,1:T(8,128)(2,1)}), bf16[2,8,32,1152]{3,2,0,1:T(8,128)(2,1)}, u32[]{:S(2)}, u32[]{:S(2)}) async-start(bf16[2,8,32,1152]{3,2,0,1:T(8,128)(2,1)} %reshape.210), calls=%async_computation.6 | async-start | bytes 2359296 | tf_op jit(solution)/shard_map/all_to_all | solution.py:115
  205.9 8.3 %convert_bitcast_fusion.2 = bf16[2,8,32,16,72]{4,1,3,2,0:T(8,128)(2,1)S(1)} fusion(bf16[2,8,32,16,72]{4,3,0,2,1:T(8,128)(2,1)} %reshape.215, f32[2,32,16,8,8]{3,4,2,1,0:T(8,128)} %get-tuple-element.35, f32[2,32,16,8]{3,2,1,0:T(8,128)} %copy-done.8, f32[2,32,16,8,8]{3,4,2,1,0:T(8,128)} %get-tuple-element.33, f32[2,32,16,8]{3,2,1,0:T(8,128)S(1)} %get-tuple-element.32), kind=kOutput, calls=%fused_computation.16 | convolution fusion | flops 57475072 | bytes 2949120 | tf_op jit(solution)/shard_map/vmap(phft,tphd->fphd)/dot_general | solution.py:52
  214.1 1.8 copy.134
  215.9 4.6 %reshape.209 = bf16[2,8,32,1152]{3,2,0,1:T(8,128)(2,1)} reshape(bf16[2,8,32,16,72]{4,3,2,0,1:T(8,128)(2,1)} %copy.134) | data formatting | bytes 2359296 | tf_op jit(solution)/shard_map/vmap()/convert_element_type | solution.py:60
  220.5 2.2 all-to-all-done.6
  222.7 4.3 %all-to-all-start.5 = ((bf16[2,8,32,1152]{3,2,0,1:T(8,128)(2,1)}), bf16[2,8,32,1152]{3,2,0,1:T(8,128)(2,1)}, u32[]{:S(2)}, u32[]{:S(2)}) async-start(bf16[2,8,32,1152]{3,2,0,1:T(8,128)(2,1)} %reshape.209), calls=%async_computation.5 | async-start | bytes 2359296 | tf_op jit(solution)/shard_map/all_to_all | solution.py:114
  227.0 0.0 all-reduce.2.cloned.1.call-start
  227.0 0.0 reduce-scatter.4.cloned.1.call-done
  227.0 2.5 copy.138
  229.5 0.0 all-reduce.2.cloned.1.call-update
  229.5 2.4 copy.126
  231.9 2.4 copy.122
  234.3 9.5 %all-to-all-done.5 = bf16[2,8,32,1152]{3,2,0,1:T(8,128)(2,1)} async-done(((bf16[2,8,32,1152]{3,2,0,1:T(8,128)(2,1)}), bf16[2,8,32,1152]{3,2,0,1:T(8,128)(2,1)}, u32[]{:S(2)}, u32[]{:S(2)}) %all-to-all-start.5) | async-done | bytes 1179680 | tf_op jit(solution)/shard_map/all_to_all | solution.py:114
  243.8 2.5 copy.118
  246.2 2.9 convolution_convert_fusion
  249.2 39.1 %all-reduce.2.cloned.1.call-done = f32[144,1152]{0,1:T(8,128)} async-done(((f32[144,1152]{0,1:T(8,128)}), f32[144,1152]{0,1:T(8,128)}) %all-reduce.2.cloned.1.call-update) | async-done | bytes 663568 | tf_op jit(solution)/shard_map/psum | solution.py:75
  288.3 2.4 copy.131
  (14 shorter events, 0.0 us)
Async XLA Ops:
  7.2 124.8 %copy-start = (bf16[1152,1152]{1,0:T(8,128)(2,1)S(1)}, bf16[1152,1152]{1,0:T(8,128)(2,1)}, u32[]{:S(2)}) copy-start(bf16[1152,1152]{1,0:T(8,128)(2,1)} %param.11) | copy-start | bytes 7962628
  10.8 22.1 %all-to-all-start = ((bf16[2,1,256,1152]{3,0,1,2:T(2,128)(2,1)}), bf16[2,1,256,1152]{3,0,1,2:T(2,128)(2,1)}, u32[]{:S(2)}, u32[]{:S(2)}) async-start(bf16[2,1,256,1152]{3,0,1,2:T(2,128)(2,1)} %copy.97), calls=%async_computation | async-start | bytes 2359296 | tf_op jit(solution)/shard_map/all_to_all | solution.py:82
  32.9 21.1 %all-to-all-start.1 = ((bf16[2,1,256,1152]{3,0,1,2:T(2,128)(2,1)}), bf16[2,1,256,1152]{3,0,1,2:T(2,128)(2,1)}, u32[]{:S(2)}, u32[]{:S(2)}) async-start(bf16[2,1,256,1152]{3,0,1,2:T(2,128)(2,1)} %copy.99), calls=%async_computation.1 | async-start | bytes 2359296 | tf_op jit(solution)/shard_map/all_to_all | solution.py:83
  37.2 21.3 %copy-start.6 = (s32[2]{0:T(128)S(1)}, s32[2]{0:T(128)}, u32[]{:S(2)}) copy-start(s32[2]{0:T(128)} %param.13) | copy-start | bytes 28
  37.2 21.3 %copy-start.5 = (s32[2]{0:T(128)S(1)}, s32[2]{0:T(128)}, u32[]{:S(2)}) copy-start(s32[2]{0:T(128)} %param.12) | copy-start | bytes 28
  54.0 26.5 %all-to-all-start.2 = ((bf16[2,1,256,1152]{3,0,1,2:T(2,128)(2,1)}), bf16[2,1,256,1152]{3,0,1,2:T(2,128)(2,1)}, u32[]{:S(2)}, u32[]{:S(2)}) async-start(bf16[2,1,256,1152]{3,0,1,2:T(2,128)(2,1)} %copy.103), calls=%async_computation.2 | async-start | bytes 2359296 | tf_op jit(solution)/shard_map/all_to_all | solution.py:84
  58.2 168.8 %reduce-scatter.4.cloned.1.call-start = ((), (), s32[]{:S(2)}) async-start(), calls=%async_computation.10 | async-start | bytes 5971968
  99.0 21.9 %copy-start.4 = (bf16[2,1,256,1152]{3,2,1,0:T(8,128)(2,1)S(1)}, bf16[2,1,256,1152]{3,2,1,0:T(8,128)(2,1)}, u32[]{:S(2)}) copy-start(bf16[2,1,256,1152]{3,2,1,0:T(8,128)(2,1)} %param.10) | copy-start | bytes 3538948
  119.9 1.0 copy-start.1
  173.8 27.6 %all-to-all-start.7 = ((bf16[2,8,32,1152]{3,2,0,1:T(8,128)(2,1)}), bf16[2,8,32,1152]{3,2,0,1:T(8,128)(2,1)}, u32[]{:S(2)}, u32[]{:S(2)}) async-start(bf16[2,8,32,1152]{3,2,0,1:T(8,128)(2,1)} %reshape.211), calls=%async_computation.7 | async-start | bytes 2359296 | tf_op jit(solution)/shard_map/all_to_all | solution.py:116
  178.5 9.1 %copy-start.3 = (bf16[2,8,32,16,72]{4,3,0,2,1:T(8,128)(2,1)S(1)}, bf16[2,8,32,16,72]{4,3,0,2,1:T(8,128)(2,1)}, u32[]{:S(2)}) copy-start(bf16[2,8,32,16,72]{4,3,0,2,1:T(8,128)(2,1)} %reshape.214) | copy-start | bytes 3538948
  178.5 9.1 %copy-start.7 = (f32[2,32,16,8,8]{3,4,2,1,0:T(8,128)S(1)}, f32[2,32,16,8,8]{3,4,2,1,0:T(8,128)}, u32[]{:S(2)}) copy-start(f32[2,32,16,8,8]{3,4,2,1,0:T(8,128)} %get-tuple-element.33) | copy-start | bytes 786436
  187.6 7.4 %copy-start.8 = (f32[2,32,16,8]{3,2,1,0:T(8,128)}, f32[2,32,16,8]{3,2,1,0:T(8,128)S(1)}, u32[]{:S(2)}) copy-start(f32[2,32,16,8]{3,2,1,0:T(8,128)S(1)} %get-tuple-element.34) | copy-start | bytes 98308
  201.4 21.2 %all-to-all-start.6 = ((bf16[2,8,32,1152]{3,2,0,1:T(8,128)(2,1)}), bf16[2,8,32,1152]{3,2,0,1:T(8,128)(2,1)}, u32[]{:S(2)}, u32[]{:S(2)}) async-start(bf16[2,8,32,1152]{3,2,0,1:T(8,128)(2,1)} %reshape.210), calls=%async_computation.6 | async-start | bytes 2359296 | tf_op jit(solution)/shard_map/all_to_all | solution.py:115
  222.7 21.1 %all-to-all-start.5 = ((bf16[2,8,32,1152]{3,2,0,1:T(8,128)(2,1)}), bf16[2,8,32,1152]{3,2,0,1:T(8,128)(2,1)}, u32[]{:S(2)}, u32[]{:S(2)}) async-start(bf16[2,8,32,1152]{3,2,0,1:T(8,128)(2,1)} %reshape.209), calls=%async_computation.5 | async-start | bytes 2359296 | tf_op jit(solution)/shard_map/all_to_all | solution.py:114
  227.0 61.3 %all-reduce.2.cloned.1.call-start = ((), (), s32[]{:S(2)}) async-start(), calls=%async_computation.9 | async-start | bytes 2359296 | tf_op jit(solution)/shard_map/psum | solution.py:75
  243.8 2.5 copy-start.2
Sparse Core Ops, SparseCore 0:
  132.0 65.7 reduce-scatter.3
  230.2 58.0 all-reduce.1
where the time goes:
time: 303 us; the launch traced here: 298 us
  local copies, waits for them, and re-layouts  83.8 us (28%)
  waiting for transfers between devices  77.5 us (26%)
  matrix products  52.3 us (17%)
  blocking collectives  40.6 us (13%)
  starting transfers between devices  27.3 us (9%)
  between operations  14.4 us (5%)
    psum x1, waiting for transfers between devices, reduce_weight(): return lax.psum(mine, 'rep')  39.1 us
    unnamed x24, local copies, waits for them, and re-layouts  23.5 us
    all_to_all x1, blocking collectives, shards(): lax.all_to_all(attn_pos, 'seq', split_axis=1, concat_axis=2, tiled=True)  20.7 us
    all_to_all x1, blocking collectives, shards(): lax.all_to_all(out_cot, 'seq', split_axis=2, concat_axis=1, tiled=True)  19.9 us
    all_to_all x1, waiting for transfers between devices, shards(): lax.all_to_all(query_rows, 'seq', split_axis=2, concat_axis=1, tiled=True)  13.4 us
    all_to_all x1, waiting for transfers between devices, shards(): lax.all_to_all(key_rows, 'seq', split_axis=2, concat_axis=1, tiled=True)  13.3 us
    all_to_all x1, waiting for transfers between devices, shards(): lax.all_to_all(grad_query_pos, 'seq', split_axis=1, concat_axis=2, tiled=...  9.45 us
    dot_general x1, matrix products, attend_back(): jnp.einsum('fphd,tphd->phft', cot_heads, value_heads, preferred_element_t...  9.06 us
  transfers between devices with their start and end apart: 8, of which 5 were waited for; matrix products, arithmetic and copies ran while one was open for 34% of the time, Pallas kernels for 0%

commit v1 on v0

v1 whole, which is shorter than its diff:
```python
import functools
import math

import jax
import jax.numpy as jnp
from jax import lax
from jax.experimental import pallas as pl
from jax.experimental.pallas import tpu as pltpu
from jax.sharding import PartitionSpec as P


HEADS = 16
LANES = 128
SUB = 16
VMEM = 60 * 1024 * 1024


def dot(a, b, ca, cb):
    return lax.dot_general(a, b, (((ca,), (cb,)), ((), ())), preferred_element_type=jnp.float32)


def pack_kernel(n, clip, *refs):
    ntensor = 4
    ins, outs = refs[:ntensor], refs[ntensor : ntensor + n]
    buf, sem_in, sem_out = refs[ntensor + n :]
    rank = lax.axis_index("seq")
    part = buf.shape[2]
    reads, writes = [], []
    for k in range(n):
        start = pl.multiple_of((rank ^ k) * part, part)
        for i, ref in enumerate(ins):
            copy = pltpu.make_async_copy(
                ref.at[clip, 0, pl.ds(start, part), :], buf.at[k, i], sem_in.at[k, i]
            )
            copy.start()
            reads.append(copy)
    for k in range(n):
        for i in range(ntensor):
            reads[k * ntensor + i].wait()
        copy = pltpu.make_async_copy(buf.at[k], outs[k], sem_out.at[k])
        copy.start()
        writes.append(copy)
    for copy in writes:
        copy.wait()


def pack(n, clip, tensors):
    _, _, npos, width = tensors[0].shape
    part = npos // n
    block = jax.ShapeDtypeStruct((4, part, width), jnp.bfloat16)
    return pl.pallas_call(
        functools.partial(pack_kernel, n, clip),
        out_shape=[block] * n,
        in_specs=[pl.BlockSpec(memory_space=pl.ANY)] * 4,
        out_specs=[pl.BlockSpec(memory_space=pl.ANY)] * n,
        scratch_shapes=[
            pltpu.VMEM((n, 4, part, width), jnp.bfloat16),
            pltpu.SemaphoreType.DMA((n, 4)),
            pltpu.SemaphoreType.DMA((n,)),
        ],
        compiler_params=pltpu.CompilerParams(vmem_limit_bytes=VMEM),
        name="pack",
    )(*tensors)


def unpack_kernel(n, clip, nprior, *refs):
    ins = refs[:n]
    outs = refs[n + nprior : n + nprior + 4]
    buf, sem_in, sem_out = refs[n + nprior + 4 :]
    rank = lax.axis_index("seq")
    part = buf.shape[2]
    reads, writes = [], []
    for k in range(n):
        copy = pltpu.make_async_copy(ins[k], buf.at[k], sem_in.at[k])
        copy.start()
        reads.append(copy)
    for k in range(n):
        reads[k].wait()
        start = pl.multiple_of((rank ^ k) * part, part)
        for i, ref in enumerate(outs):
            copy = pltpu.make_async_copy(
                buf.at[k, i], ref.at[clip, 0, pl.ds(start, part), :], sem_out.at[k, i]
            )
            copy.start()
            writes.append(copy)
    for copy in writes:
        copy.wait()


def unpack(n, clip, full, blocks, prior):
    part, width = blocks[0].shape[1:]
    nprior = len(prior)
    return pl.pallas_call(
        functools.partial(unpack_kernel, n, clip, nprior),
        out_shape=[jax.ShapeDtypeStruct(full, jnp.bfloat16)] * 4,
        in_specs=[pl.BlockSpec(memory_space=pl.ANY)] * (n + nprior),
        out_specs=[pl.BlockSpec(memory_space=pl.ANY)] * 4,
        input_output_aliases={n + i: i for i in range(nprior)},
        scratch_shapes=[
            pltpu.VMEM((n, 4, part, width), jnp.bfloat16),
            pltpu.SemaphoreType.DMA((n,)),
            pltpu.SemaphoreType.DMA((n, 4)),
        ],
        compiler_params=pltpu.CompilerParams(vmem_limit_bytes=VMEM),
        name="unpack",
    )(*blocks, *prior)


def attend_kernel(n, clip, last, nprior, frames_ref, places_ref, *refs):
    ins, weight_ref = refs[:n], refs[n]
    prior = refs[n + 1 : n + 1 + nprior]
    refs = refs[n + 1 + nprior :]
    outs, refs = refs[:n], refs[n:]
    wgrads, refs = refs[: 1 + last], refs[1 + last :]
    q_s, k_s, v_s, g_s, c_s, o_s, dq_s, dk_s, dv_s, pr_s, w_s, gw_s = refs[:12]
    sem_in, sem_w, sem_out, sem_gw = refs[12:]
    rank = lax.axis_index("seq")
    part, width = ins[0].shape[1:]
    nblock = part // SUB
    rows = n * SUB
    head_dim = width // HEADS
    inv_root = 1.0 / math.sqrt(head_dim)
    nframe_live = frames_ref[clip]
    nplace_live = places_ref[clip]

    reads = {}
    for i, ref in ((3, g_s), (0, q_s), (1, k_s), (2, v_s)):
        reads[i] = [
            pltpu.make_async_copy(
                ins[k].at[i, pl.ds(b * SUB, SUB), :],
                ref.at[b, pl.ds(k * SUB, SUB), :],
                sem_in.at[i, b, k],
            )
            for b in range(nblock)
            for k in range(n)
        ]
    weight_read = pltpu.make_async_copy(weight_ref, w_s, sem_w.at[0])
    weight_read.start()
    for i in (3, 0, 1, 2):
        for copy in reads[i]:
            copy.start()
    prior_reads = [pltpu.make_async_copy(ref, gw_s, sem_w.at[1]) for ref in prior]
    for copy in prior_reads:
        copy.start()

    row_id = lax.broadcasted_iota(jnp.int32, (rows, 1), 0)
    col_id = lax.broadcasted_iota(jnp.int32, (1, rows), 1)
    row_alive = ((row_id // SUB) ^ rank) < nframe_live
    key_alive = ((col_id // SUB) ^ rank) < nframe_live
    allowed = ((row_id % SUB) == (col_id % SUB)) & key_alive

    def live(b):
        place = rank * part + b * SUB + row_id % SUB
        return row_alive & (place < nplace_live)

    weight_read.wait()
    for copy in reads[3]:
        copy.wait()
    for b in range(nblock):
        cot = dot(g_s[b], w_s[...], 1, 0)
        c_s[b] = jnp.where(live(b), cot, 0.0).astype(jnp.bfloat16)
    for i in (0, 1, 2):
        for copy in reads[i]:
            copy.wait()

    window_lane = lax.broadcasted_iota(jnp.int32, (1, 2 * LANES), 1)

    def pairs(b, carry):
        alive = live(b)
        for j in range(HEADS // 2):
            lanes = slice(j * LANES, (j + 2) * LANES)
            first = 2 * head_dim * j - LANES * j
            own = [
                (window_lane >= first + h * head_dim) & (window_lane < first + (h + 1) * head_dim)
                for h in range(2)
            ]

            def both(x):
                zero = jnp.zeros_like(x)
                return jnp.concatenate([jnp.where(m, x, zero) for m in own], axis=0)

            qw, kw, vw, cw = q_s[b, :, lanes], k_s[b, :, lanes], v_s[b, :, lanes], c_s[b, :, lanes]
            q2, k2, v2, c2 = both(qw), both(kw), both(vw), both(cw)
            scores = dot(qw, k2, 1, 1)
            gattns = dot(cw, v2, 1, 1)
            rounded, high, low = [], [], []
            for h in range(2):
                part_of = slice(h * rows, (h + 1) * rows)
                score = jnp.where(allowed, scores[:, part_of] * inv_root, -1e30)
                expo = jnp.exp(score - jnp.max(score, axis=1, keepdims=True))
                weights = expo / jnp.sum(expo, axis=1, keepdims=True)
                rounded.append(weights.astype(jnp.bfloat16))
                gattn = gattns[:, part_of]
                delta = jnp.sum(weights * gattn, axis=1, keepdims=True)
                gscore = weights * (gattn - delta) * inv_root
                high.append(gscore.astype(jnp.bfloat16))
                low.append((gscore - high[h].astype(jnp.float32)).astype(jnp.bfloat16))
            across = [jnp.concatenate(x, axis=1) for x in (rounded, high, low)]
            down = [jnp.concatenate(x, axis=0) for x in (rounded, high, low)]
            out = jnp.where(alive, dot(across[0], v2, 1, 0), 0.0)
            dq = dot(across[1], k2, 1, 0) + dot(across[2], k2, 1, 0)
            dv = dot(down[0], c2, 0, 0)
            dk = dot(down[1], q2, 0, 0) + dot(down[2], q2, 0, 0)
            mine = window_lane[:, :LANES] >= first
            lead = slice(j * LANES, (j + 1) * LANES)
            tail = slice((j + 1) * LANES, (j + 2) * LANES)
            for ref, value in ((o_s, out), (dq_s, dq), (dk_s, dk), (dv_s, dv)):
                value = value.astype(jnp.bfloat16)
                if j:
                    ref[b, :, lead] = jnp.where(mine, value[:, :LANES], ref[b, :, lead])
                else:
                    ref[b, :, lead] = value[:, :LANES]
                ref[b, :, tail] = value[:, LANES:]
        return carry

    lax.fori_loop(0, nblock, pairs, 0)

    writes = []

    def send(i, ref):
        for k in range(n):
            for b in range(nblock):
                copy = pltpu.make_async_copy(
                    ref.at[b, pl.ds(k * SUB, SUB), :],
                    outs[k].at[i, pl.ds(b * SUB, SUB), :],
                    sem_out.at[i, b, k],
                )
                copy.start()
                writes.append(copy)

    for i, ref in ((1, dq_s), (2, dk_s), (3, dv_s)):
        send(i, ref)
    for copy in prior_reads:
        copy.wait()
    tile = width // 3
    for i in range(3):
        cols = slice(i * tile, (i + 1) * tile)
        total = gw_s[cols, :] if nprior else 0.0
        for b in range(nblock):
            total = total + dot(g_s[b, :, cols], o_s[b], 0, 0)
        gw_s[cols, :] = total
    if last:
        half, count = n // 2, width // n
        give, keep = wgrads
        core = rank % 2
        for m in range(half):
            there = pl.multiple_of((2 * m + 1 - core) * count, 8)
            give[m] = gw_s[pl.ds(there, count), :].astype(jnp.bfloat16)
            here = pl.multiple_of((2 * m + core) * count, 8)
            copy = pltpu.make_async_copy(gw_s.at[pl.ds(here, count), :], keep.at[m], sem_gw.at[m])
            copy.start()
            writes.append(copy)
    else:
        copy = pltpu.make_async_copy(gw_s, wgrads[0], sem_gw.at[0])
        copy.start()
        writes.append(copy)
    for b in range(nblock):
        pr_s[b] = dot(o_s[b], w_s[...], 1, 1).astype(jnp.bfloat16)
    send(0, pr_s)
    for copy in writes:
        copy.wait()


def attend(n, clip, last, frame_count, pos_count, blocks, weight, prior):
    part, width = blocks[0].shape[1:]
    nblock, rows = part // SUB, n * SUB
    vmem = pl.BlockSpec(memory_space=pltpu.VMEM)
    smem = pl.BlockSpec(memory_space=pltpu.SMEM)
    hbm = pl.BlockSpec(memory_space=pl.ANY)
    nprior = len(prior)
    block = jax.ShapeDtypeStruct((4, part, width), jnp.bfloat16)
    if last:
        halves = (n // 2, width // n, width)
        wgrads = [jax.ShapeDtypeStruct(halves, t) for t in (jnp.bfloat16, jnp.float32)]
        wspecs = [vmem, hbm]
    else:
        wgrads, wspecs = [jax.ShapeDtypeStruct((width, width), jnp.float32)], [hbm]
    return pl.pallas_call(
        functools.partial(attend_kernel, n, clip, last, nprior),
        out_shape=[block] * n + wgrads,
        in_specs=[smem, smem] + [hbm] * (n + 1 + nprior),
        out_specs=[hbm] * n + wspecs,
        scratch_shapes=[pltpu.VMEM((nblock, rows, width), jnp.bfloat16)] * 10
        + [
            pltpu.VMEM((width, width), jnp.bfloat16),
            pltpu.VMEM((width, width), jnp.float32),
            pltpu.SemaphoreType.DMA((4, nblock, n)),
            pltpu.SemaphoreType.DMA((2,)),
            pltpu.SemaphoreType.DMA((4, nblock, n)),
            pltpu.SemaphoreType.DMA((n // 2,)),
        ],
        compiler_params=pltpu.CompilerParams(vmem_limit_bytes=VMEM),
        cost_estimate=pl.CostEstimate(
            flops=10_000_000_000, bytes_accessed=16_000_000, transcendentals=0
        ),
        name="attend",
    )(frame_count, pos_count, *blocks, weight, *prior)


def small_call(kernel, out_shape, args, scratch=()):
    vmem = pl.BlockSpec(memory_space=pltpu.VMEM)
    return pl.pallas_call(
        kernel,
        out_shape=out_shape,
        in_specs=[vmem] * len(args),
        out_specs=[vmem] * len(out_shape),
        scratch_shapes=list(scratch),
        compiler_params=pltpu.CompilerParams(vmem_limit_bytes=VMEM),
        cost_estimate=pl.CostEstimate(
            flops=1_000_000_000, bytes_accessed=4_000_000, transcendentals=0
        ),
    )(*args)


def chip_sum_kernel(half, keep, came, own, *outs):
    chip = lax.axis_index("seq") // 2
    own[...] = keep[chip] + came[chip].astype(jnp.float32)
    for q in range(1, half):
        outs[q - 1][...] = (keep[chip ^ q] + came[chip ^ q].astype(jnp.float32)).astype(jnp.bfloat16)


def plane_sum_kernel(half, nrep, own, *refs):
    came, mine, outs, acc = refs[: half - 1], refs[half - 1], refs[half:-1], refs[-1]
    plane = lax.axis_index("rep")
    count, share = own.shape[0], mine.shape[0]
    acc[...] = jnp.zeros_like(acc)
    total = own[...]
    for ref in came:
        total = total + ref[...].astype(jnp.float32)
    acc[:count, :] = total
    mine[...] = acc[pl.ds(pl.multiple_of(plane * share, 8), share), :]
    for w in range(1, nrep):
        there = pl.multiple_of((plane ^ w) * share, 8)
        outs[w - 1][...] = acc[pl.ds(there, share), :].astype(jnp.bfloat16)


def replica_sum_kernel(mine, *refs):
    total = mine[...]
    for ref in refs[:-1]:
        total = total + ref[...].astype(jnp.float32)
    refs[-1][...] = total.astype(jnp.bfloat16)


def assemble_kernel(nrep, *refs):
    parts, out, acc = refs[:nrep], refs[-2], refs[-1]
    plane = lax.axis_index("rep")
    share = parts[0].shape[0]
    for w in range(nrep):
        there = pl.multiple_of((plane ^ w) * share, 8)
        acc[pl.ds(there, share), :] = parts[w][...].astype(jnp.float32)
    out[...] = acc[: out.shape[0], :]


def permute(x, axis, size, step):
    return lax.ppermute(x, axis, [(i, i ^ step) for i in range(size)])


def exchange(n, order, blocks):
    moved = [None] * n
    moved[0] = blocks[0]
    for k in order:
        moved[k] = permute(blocks[k], "seq", n, k)
    return moved


def reduce_weight(n, nrep, give, keep):
    half, count, width = keep.shape
    came = permute(give, "seq", n, 1)
    wide = jax.ShapeDtypeStruct((count, width), jnp.float32)
    narrow = jax.ShapeDtypeStruct((count, width), jnp.bfloat16)
    own, *sends = small_call(
        functools.partial(chip_sum_kernel, half), [wide] + [narrow] * (half - 1), [keep, came]
    )
    came = [permute(sends[q - 1], "seq", n, 2 * q) for q in range(1, half)]
    share = -(-(-(-count // nrep)) // 8) * 8
    acc = pltpu.VMEM((nrep * share, width), jnp.float32)
    wide = jax.ShapeDtypeStruct((share, width), jnp.float32)
    narrow = jax.ShapeDtypeStruct((share, width), jnp.bfloat16)
    mine, *sends = small_call(
        functools.partial(plane_sum_kernel, half, nrep),
        [wide] + [narrow] * (nrep - 1),
        [own, *came],
        [acc],
    )
    came = [permute(sends[w - 1], "rep", nrep, w) for w in range(1, nrep)]
    (mine,) = small_call(replica_sum_kernel, [narrow], [mine, *came])
    came = [permute(mine, "rep", nrep, w) for w in range(1, nrep)]
    (out,) = small_call(
        functools.partial(assemble_kernel, nrep),
        [jax.ShapeDtypeStruct((count, width), jnp.float32)],
        [mine, *came],
        [acc],
    )
    return out


def send_order(n):
    return sorted(range(1, n), key=lambda k: (k < 2, -bin(k >> 1).count("1"), k))


def shards(n, nrep, query_rows, key_rows, value_rows, out_grad, out_weight, frame_count, pos_count):
    nclip, frame_local, npos, _ = query_rows.shape
    if frame_local != 1 or n & (n - 1) or nrep & (nrep - 1) or (npos // n) % SUB:
        raise ValueError("sizes")
    order = send_order(n)
    tensors = (query_rows, key_rows, value_rows, out_grad)
    arrived = [exchange(n, order, pack(n, c, tensors)) for c in range(nclip)]
    prior, back = (), []
    for c in range(nclip):
        last = c == nclip - 1
        done = attend(n, c, last, frame_count, pos_count, arrived[c], out_weight, prior)
        blocks, prior = done[:n], tuple(done[n:])
        back.append(exchange(n, order, blocks))
    wgrad = reduce_weight(n, nrep, *prior)
    outs = ()
    for c in range(nclip):
        outs = unpack(n, c, query_rows.shape, back[c], outs)
    return (*outs, wgrad)


def solution(mesh):
    n, nrep = mesh.shape["seq"], mesh.shape["rep"]
    rows = P("rep", "seq", None, None)
    return jax.shard_map(
        functools.partial(shards, n, nrep),
        mesh=mesh,
        in_specs=(rows, rows, rows, rows, P(), P("rep"), P("rep")),
        out_specs=(rows, rows, rows, rows, P("seq", None)),
        check_vma=False,
    )
```

time: 303 us -> 183 us (0.60); the launches traced: 298 us -> 183 us
  local copies, waits for them, and re-layouts: 83.8 us -> 4.21 us
  Pallas kernels: 0 us -> 58.9 us
  matrix products: 52.3 us -> 0 us
  blocking collectives: 40.6 us -> 0 us
  starting transfers between devices: 27.3 us -> 51.1 us
  between operations: 14.4 us -> 1.02 us
  waiting for transfers between devices: 77.5 us -> 67.4 us
    ppermute x0 -> x38, waiting for transfers between devices: none -> 67.4 us  [permute(): return lax.ppermute(x, axis, [(i, i ^ step) for i in range(size)])]
    pallas_call x0 -> x10, Pallas kernels: none -> 58.9 us  [the longest x2 38.1 us: attend(): pl.pallas_call(functools.partial(attend_kernel, n, clip, last, nprior), o...]
    ppermute x0 -> x38, starting transfers between devices: none -> 51.1 us  [permute(): return lax.ppermute(x, axis, [(i, i ^ step) for i in range(size)])]
    dot_general x8 -> x0, matrix products: 43.6 us -> none  [the longest x1 9.06 us: attend_back(): jnp.einsum('fphd,tphd->phft', cot_heads, value_heads, preferred_element_t...]
    all_to_all x2 -> x0, blocking collectives: 40.6 us -> none  [the longest x1 20.7 us: shards(): lax.all_to_all(attn_pos, 'seq', split_axis=1, concat_axis=2, tiled=True)]
    psum x1 -> x0, waiting for transfers between devices: 39.1 us -> none  [reduce_weight(): return lax.psum(mine, 'rep')]
    all_to_all x6 -> x0, waiting for transfers between devices: 38.3 us -> none  [the longest x1 13.4 us: shards(): lax.all_to_all(query_rows, 'seq', split_axis=2, concat_axis=1, tiled=True)]
    reshape x5 -> x0, local copies, waits for them, and re-layouts: 30.7 us -> none  [the longest x1 6.53 us: attend_local(): value_heads = value_part.reshape(shape_heads)]
  transfers between devices with their start and end apart: 8 -> 38, of which waited for: 5 -> 12; matrix products, arithmetic and copies ran while one was open for 34% -> 0% of each run, Pallas kernels for 0% -> 19%
where the time goes in v1:
time: 183 us
  waiting for transfers between devices  67.4 us (37%)
  Pallas kernels  58.9 us (32%)
  starting transfers between devices  51.1 us (28%)
  local copies, waits for them, and re-layouts  4.21 us (2%)
    ppermute x38, waiting for transfers between devices, permute(): return lax.ppermute(x, axis, [(i, i ^ step) for i in range(size)])  67.4 us
    ppermute x38, starting transfers between devices, permute(): return lax.ppermute(x, axis, [(i, i ^ step) for i in range(size)])  51.1 us
    pallas_call x2, Pallas kernels, attend(): pl.pallas_call(functools.partial(attend_kernel, n, clip, last, nprior), o...  38.1 us
    pallas_call x4, Pallas kernels, small_call(): pl.pallas_call(kernel, out_shape=out_shape, in_specs=[vmem] * len(args),...  9.67 us
    pallas_call x2, Pallas kernels, pack(): pl.pallas_call(functools.partial(pack_kernel, n, clip), out_shape=[block]...  5.69 us
    pallas_call x2, Pallas kernels, unpack(): pl.pallas_call(functools.partial(unpack_kernel, n, clip, nprior), out_sha...  5.4 us
    unnamed x84, local copies, waits for them, and re-layouts  4.21 us
  transfers between devices with their start and end apart: 38, of which 12 were waited for; matrix products, arithmetic and copies ran while one was open for 0% of the time, Pallas kernels for 19%

profile of v1, /device:TPU:0, one launch (start us, length us, event | category | flops | bytes accessed | tf_op | source)
XLA Modules:
  0.0 182.5 jit_solution(14345080834945968373)
XLA Ops:
  0.6 2.8 %pack.3 = (bf16[4,32,1152]{2,1,0:T(8,128)(2,1)}, bf16[4,32,1152]{2,1,0:T(8,128)(2,1)}, bf16[4,32,1152]{2,1,0:T(8,128)(2,1)}, bf16[4,32,1152]{2,1,0:T(8,128)(2,1)...) custom-call(bf16[2,1,256,1152]{3,2,1,0:T(8,128)(2,1)} %refs_0_.3, ...), custom_call_target="tpu_custom_call" | custom-call | tf_op jit(solution)/shard_map/pack/pallas_call | solution.py:51
  3.5 0.6 collective-permute-start.7
  4.0 2.6 %collective-permute-start.8 = (bf16[4,32,1152]{2,1,0:T(8,128)(2,1)}, bf16[4,32,1152]{2,1,0:T(8,128)(2,1)S(1)}, u32[]{:S(2)}, u32[]{:S(2)}) collective-permute-start(bf16[4,32,1152]{2,1,0:T(8,128)(2,1)} %get-tuple-element.66), channel_id=1, source_target_pairs={{0,8},{4,12},{8,0},{12,4},{16,24},{20,28},{24,16},{28,20},{1,9},{5... | collective-permute-start | bytes 884744 | tf_op jit(solution)/shard_map/ppermute | solution.py:355
  6.6 1.8 collective-permute-start.10
  8.4 2.9 %pack.2 = (bf16[4,32,1152]{2,1,0:T(8,128)(2,1)}, bf16[4,32,1152]{2,1,0:T(8,128)(2,1)}, bf16[4,32,1152]{2,1,0:T(8,128)(2,1)}, bf16[4,32,1152]{2,1,0:T(8,128)(2,1)...) custom-call(bf16[2,1,256,1152]{3,2,1,0:T(8,128)(2,1)} %refs_0_.3, ...), custom_call_target="tpu_custom_call" | custom-call | tf_op jit(solution)/shard_map/pack/pallas_call | solution.py:51
  11.3 2.6 %collective-permute-start.12 = (bf16[4,32,1152]{2,1,0:T(8,128)(2,1)S(1)}, bf16[4,32,1152]{2,1,0:T(8,128)(2,1)S(1)}, u32[]{:S(2)}, u32[]{:S(2)}) collective-permute-start(bf16[4,32,1152]{2,1,0:T(8,128)(2,1)S(1)} %copy-done.32), channel_id=1, source_target_pairs={{0,24},{4,28},{8,16},{12,20},{16,8},{20,12},{24,0},{28,4},{1,25},{... | collective-permute-start | bytes 884744 | tf_op jit(solution)/shard_map/ppermute | solution.py:355
  13.9 0.7 collective-permute-done.8.refs_2_
  14.7 1.6 collective-permute-start.13
  16.3 4.3 %collective-permute-done.9.refs_3_ = bf16[4,32,1152]{2,1,0:T(8,128)(2,1)S(1)} collective-permute-done((bf16[4,32,1152]{2,1,0:T(8,128)(2,1)}, bf16[4,32,1152]{2,1,0:T(8,128)(2,1)S(1)}, u32[]{:S(2)}, u32[]{:S(2)}) %collective-permute-start.9) | collective-permute-done | bytes 294944 | tf_op jit(solution)/shard_map/ppermute | solution.py:355
  20.6 0.5 collective-permute-start
  21.1 2.0 %collective-permute-start.1 = (bf16[4,32,1152]{2,1,0:T(8,128)(2,1)}, bf16[4,32,1152]{2,1,0:T(8,128)(2,1)S(1)}, u32[]{:S(2)}, u32[]{:S(2)}) collective-permute-start(bf16[4,32,1152]{2,1,0:T(8,128)(2,1)} %get-tuple-element.58), channel_id=1, source_target_pairs={{0,8},{4,12},{8,0},{12,4},{16,24},{20,28},{24,16},{28,20},{1,9},{5... | collective-permute-start | bytes 884744 | tf_op jit(solution)/shard_map/ppermute | solution.py:355
  23.1 11.3 %collective-permute-done.11.refs_5_ = bf16[4,32,1152]{2,1,0:T(8,128)(2,1)S(1)} collective-permute-done((bf16[4,32,1152]{2,1,0:T(8,128)(2,1)}, bf16[4,32,1152]{2,1,0:T(8,128)(2,1)S(1)}, u32[]{:S(2)}, u32[]{:S(2)}) %collective-permute-start.11) | collective-permute-done | bytes 294944 | tf_op jit(solution)/shard_map/ppermute | solution.py:355
  34.5 2.1 %collective-permute-start.2 = (bf16[4,32,1152]{2,1,0:T(8,128)(2,1)}, bf16[4,32,1152]{2,1,0:T(8,128)(2,1)S(1)}, u32[]{:S(2)}, u32[]{:S(2)}) collective-permute-start(bf16[4,32,1152]{2,1,0:T(8,128)(2,1)} %get-tuple-element.59), channel_id=1, source_target_pairs={{0,12},{4,8},{8,4},{12,0},{16,28},{20,24},{24,20},{28,16},{1,13},{... | collective-permute-start | bytes 884744 | tf_op jit(solution)/shard_map/ppermute | solution.py:355
  36.5 1.5 collective-permute-start.3
  38.1 1.2 collective-permute-start.5
  39.3 0.6 collective-permute-done.1.refs_2_
  40.0 1.6 collective-permute-start.6
  41.6 18.3 %attend.2 = (bf16[4,32,1152]{2,1,0:T(8,128)(2,1)}, bf16[4,32,1152]{2,1,0:T(8,128)(2,1)}, bf16[4,32,1152]{2,1,0:T(8,128)(2,1)}, bf16[4,32,1152]{2,1,0:T(8,128)(2,...) custom-call(s32[2]{0:T(128)} %frames_ref.3, ...), custom_call_target="tpu_custom_call" | custom-call | flops 10000000000 | bytes 16000000 | tf_op jit(solution)/shard_map/attend/pallas_call | solution.py:278
  60.0 3.6 %collective-permute-done.4.refs_5_ = bf16[4,32,1152]{2,1,0:T(8,128)(2,1)S(1)} collective-permute-done((bf16[4,32,1152]{2,1,0:T(8,128)(2,1)}, bf16[4,32,1152]{2,1,0:T(8,128)(2,1)S(1)}, u32[]{:S(2)}, u32[]{:S(2)}) %collective-permute-start.4) | collective-permute-done | bytes 294944 | tf_op jit(solution)/shard_map/ppermute | solution.py:355
  63.6 0.7 copy-done.33
  64.3 0.1 copy-done.34
  64.4 0.1 copy-done.35
  64.5 19.8 %attend.3 = (bf16[4,32,1152]{2,1,0:T(8,128)(2,1)}, bf16[4,32,1152]{2,1,0:T(8,128)(2,1)}, bf16[4,32,1152]{2,1,0:T(8,128)(2,1)}, bf16[4,32,1152]{2,1,0:T(8,128)(2,...) custom-call(s32[2]{0:T(128)} %frames_ref.3, ...), custom_call_target="tpu_custom_call" | custom-call | flops 10000000000 | bytes 16000000 | tf_op jit(solution)/shard_map/attend/pallas_call | solution.py:278
  84.3 0.5 collective-permute-start.28
  84.8 0.1 collective-permute-start.14
  84.9 0.9 collective-permute-start.15
  85.8 0.9 collective-permute-start.16
  86.7 1.0 collective-permute-done.28.came
  87.7 1.1 copy-done
  88.8 3.5 %shard_map.110 = (f32[144,1152]{1,0:T(8,128)}, bf16[144,1152]{1,0:T(8,128)(2,1)}, bf16[144,1152]{1,0:T(8,128)(2,1)}, bf16[144,1152]{1,0:T(8,128)(2,1)}) custom-call(f32[4,144,1152]{2,1,0:T(8,128)} %get-tuple-element.97.keep, bf16[4,144,1152]{2,1,0:T(8,128)(2,1)} %copy-done), custom_call_target="tpu_custom_call" | custom-call | flops 1000000000 | bytes 4000000 | tf_op jit(solution)/shard_map/pallas_call | solution.py:302
  92.3 0.9 collective-permute-start.29
  93.3 1.5 collective-permute-start.30
  94.8 1.0 collective-permute-start.31
  95.8 1.8 collective-permute-start.17
  97.7 2.6 %collective-permute-done.16.refs_3_ = bf16[4,32,1152]{2,1,0:T(8,128)(2,1)S(1)} collective-permute-done((bf16[4,32,1152]{2,1,0:T(8,128)(2,1)}, bf16[4,32,1152]{2,1,0:T(8,128)(2,1)S(1)}, u32[]{:S(2)}, u32[]{:S(2)}) %collective-permute-start.16) | collective-permute-done | bytes 294944 | tf_op jit(solution)/shard_map/ppermute | solution.py:355
  100.2 2.5 %collective-permute-start.18 = (bf16[4,32,1152]{2,1,0:T(8,128)(2,1)}, bf16[4,32,1152]{2,1,0:T(8,128)(2,1)S(1)}, u32[]{:S(2)}, u32[]{:S(2)}) collective-permute-start(bf16[4,32,1152]{2,1,0:T(8,128)(2,1)} %get-tuple-element.78), channel_id=1, source_target_pairs={{0,20},{4,16},{8,28},{12,24},{16,4},{20,0},{24,12},{28,8},{1,21},{... | collective-permute-start | bytes 884744 | tf_op jit(solution)/shard_map/ppermute | solution.py:355
  102.8 14.8 %collective-permute-done.17.refs_4_ = bf16[4,32,1152]{2,1,0:T(8,128)(2,1)S(1)} collective-permute-done((bf16[4,32,1152]{2,1,0:T(8,128)(2,1)S(1)}, bf16[4,32,1152]{2,1,0:T(8,128)(2,1)S(1)}, u32[]{:S(2)}, u32[]{:S(2)}) %collective-permute-start.17) | collective-permute-done | bytes 294944 | tf_op jit(solution)/shard_map/ppermute | solution.py:355
  117.6 1.2 collective-permute-start.22
  118.8 0.7 collective-permute-start.23
  119.4 1.5 collective-permute-start.24
  121.0 2.4 %shard_map.111 = (f32[40,1152]{1,0:T(8,128)}, bf16[40,1152]{1,0:T(8,128)(2,1)}, bf16[40,1152]{1,0:T(8,128)(2,1)}, bf16[40,1152]{1,0:T(8,128)(2,1)}) custom-call(f32[144,1152]{1,0:T(8,128)} %get-tuple-element.99.own, bf16[144,1152]{1,0:T(8,128)(2,1)} %copy-done.15, bf16[144,1152]{1,0:T(8,128)(2,1)} %copy-done.16, bf16[144,1152]{1,0:T(8,128)(2,1)} %copy-done.17), custom_call_target="tpu_custom_call" | custom-call | flops 1000000000 | bytes 4000000 | tf_op jit(solution)/shard_map/pallas_call | solution.py:302
  123.5 1.6 collective-permute-start.32
  125.1 2.6 %collective-permute-start.33 = (bf16[40,1152]{1,0:T(8,128)(2,1)}, bf16[40,1152]{1,0:T(8,128)(2,1)S(1)}, u32[]{:S(2)}, u32[]{:S(2)}) collective-permute-start(bf16[40,1152]{1,0:T(8,128)(2,1)} %get-tuple-element.105), channel_id=1, source_target_pairs={{0,2},{1,3},{2,0},{3,1},{4,6},{5,7},{6,4},{7,5},{8,10},{9,11},{10,... | collective-permute-start | bytes 276488 | tf_op jit(solution)/shard_map/ppermute | solution.py:355
  127.7 0.1 collective-permute-done.22.refs_2_
  127.7 3.6 %collective-permute-start.34 = (bf16[40,1152]{1,0:T(8,128)(2,1)}, bf16[40,1152]{1,0:T(8,128)(2,1)S(1)}, u32[]{:S(2)}, u32[]{:S(2)}) collective-permute-start(bf16[40,1152]{1,0:T(8,128)(2,1)} %get-tuple-element.106), channel_id=1, source_target_pairs={{0,3},{1,2},{2,1},{3,0},{4,7},{5,6},{6,5},{7,4},{8,11},{9,10},{10,... | collective-permute-start | bytes 276488 | tf_op jit(solution)/shard_map/ppermute | solution.py:355
  131.4 1.6 collective-permute-done.23.refs_3_
  133.0 1.8 collective-permute-start.25
  134.8 1.0 collective-permute-start.26
  135.8 1.1 collective-permute-start.27
  137.0 1.4 collective-permute-start.19
  138.4 1.8 collective-permute-start.20
  140.2 1.7 shard_map.112.refs_0_
  141.9 25.1 %collective-permute-done.25.refs_5_ = bf16[4,32,1152]{2,1,0:T(8,128)(2,1)S(1)} collective-permute-done((bf16[4,32,1152]{2,1,0:T(8,128)(2,1)}, bf16[4,32,1152]{2,1,0:T(8,128)(2,1)S(1)}, u32[]{:S(2)}, u32[]{:S(2)}) %collective-permute-start.25) | collective-permute-done | bytes 294944 | tf_op jit(solution)/shard_map/ppermute | solution.py:355
  167.1 3.6 %collective-permute-start.37 = (bf16[40,1152]{1,0:T(8,128)(2,1)}, bf16[40,1152]{1,0:T(8,128)(2,1)S(1)}, u32[]{:S(2)}, u32[]{:S(2)}) collective-permute-start(bf16[40,1152]{1,0:T(8,128)(2,1)} %shard_map.112.refs_0_), channel_id=1, source_target_pairs={{0,3},{1,2},{2,1},{3,0},{4,7},{5,6},{6,5},{7,4},{8,11},{9,10},{10,... | collective-permute-start | bytes 276488 | tf_op jit(solution)/shard_map/ppermute | solution.py:355
  170.7 0.8 collective-permute-start.35
  171.5 0.1 copy-done.14
  171.5 2.7 %unpack.2 = (bf16[2,1,256,1152]{3,2,1,0:T(8,128)(2,1)}, bf16[2,1,256,1152]{3,2,1,0:T(8,128)(2,1)}, bf16[2,1,256,1152]{3,2,1,0:T(8,128)(2,1)}, bf16[2,1,256,1152]{3,2,1,0:T(8,128)(2,1)}) custom-call(bf16[4,32,1152]{2,1,0:T(8,128)(2,1)} %get-tuple-element.81.refs_0_, bf16[4,32,1152]{2,1,0:T(8,128)(2,1)} %copy-done.6, bf16[4,32,1152]{2,1,0:T(8,128)(2,1)} %copy-done.7, ...), custom_call_target="tpu_custom_call" | custom-call | tf_op jit(solution)/shard_map/unpack/pallas_call | solution.py:93
  174.3 0.7 copy-done.11
  175.0 0.1 copy-done.13
  175.1 2.7 %unpack.3 = (bf16[2,1,256,1152]{3,2,1,0:T(8,128)(2,1)}, bf16[2,1,256,1152]{3,2,1,0:T(8,128)(2,1)}, bf16[2,1,256,1152]{3,2,1,0:T(8,128)(2,1)}, bf16[2,1,256,1152]{3,2,1,0:T(8,128)(2,1)}) custom-call(bf16[4,32,1152]{2,1,0:T(8,128)(2,1)} %get-tuple-element.73.refs_0_, ...), custom_call_target="tpu_custom_call", output_to_operand_aliasing={{0}: (8, {}), {1}: (9, {}), {2}: (10, {}), {3}: (11, {})} | custom-call | tf_op jit(solution)/shard_map/unpack/pallas_call | solution.py:93
  177.8 1.5 collective-permute-done.36.refs_2_
  179.3 0.6 copy-done.37
  179.9 0.6 copy-done.39
  180.6 2.0 %shard_map.113 = f32[144,1152]{1,0:T(8,128)} custom-call(bf16[40,1152]{1,0:T(8,128)(2,1)} %shard_map.112.refs_0_, bf16[40,1152]{1,0:T(8,128)(2,1)} %copy-done.39, bf16[40,1152]{1,0:T(8,128)(2,1)} %copy-done.37, bf16[40,1152]{1,0:T(8,128)(2,1)} %copy-done.36), custom_call_target="tpu_custom_call" | custom-call | flops 1000000000 | bytes 4000000 | tf_op jit(solution)/shard_map/pallas_call | solution.py:302
  (106 shorter events, 0.3 us)
Async XLA Ops:
  3.5 7.8 %collective-permute-start.7 = (bf16[4,32,1152]{2,1,0:T(8,128)(2,1)}, bf16[4,32,1152]{2,1,0:T(8,128)(2,1)S(1)}, u32[]{:S(2)}, u32[]{:S(2)}) collective-permute-start(bf16[4,32,1152]{2,1,0:T(8,128)(2,1)} %get-tuple-element.65), channel_id=1, source_target_pairs={{0,4},{4,0},{8,12},{12,8},{16,20},{20,16},{24,28},{28,24},{1,5},{5... | collective-permute-start | bytes 884744 | tf_op jit(solution)/shard_map/ppermute | solution.py:355
  4.0 10.6 %collective-permute-start.8 = (bf16[4,32,1152]{2,1,0:T(8,128)(2,1)}, bf16[4,32,1152]{2,1,0:T(8,128)(2,1)S(1)}, u32[]{:S(2)}, u32[]{:S(2)}) collective-permute-start(bf16[4,32,1152]{2,1,0:T(8,128)(2,1)} %get-tuple-element.66), channel_id=1, source_target_pairs={{0,8},{4,12},{8,0},{12,4},{16,24},{20,28},{24,16},{28,20},{1,9},{5... | collective-permute-start | bytes 884744 | tf_op jit(solution)/shard_map/ppermute | solution.py:355
  6.6 14.0 %collective-permute-start.9 = (bf16[4,32,1152]{2,1,0:T(8,128)(2,1)}, bf16[4,32,1152]{2,1,0:T(8,128)(2,1)S(1)}, u32[]{:S(2)}, u32[]{:S(2)}) collective-permute-start(bf16[4,32,1152]{2,1,0:T(8,128)(2,1)} %get-tuple-element.67), channel_id=1, source_target_pairs={{0,12},{4,8},{8,4},{12,0},{16,28},{20,24},{24,20},{28,16},{1,13},{... | collective-permute-start | bytes 884744 | tf_op jit(solution)/shard_map/ppermute | solution.py:355
  6.6 14.5 %collective-permute-start.10 = (bf16[4,32,1152]{2,1,0:T(8,128)(2,1)}, bf16[4,32,1152]{2,1,0:T(8,128)(2,1)S(1)}, u32[]{:S(2)}, u32[]{:S(2)}) collective-permute-start(bf16[4,32,1152]{2,1,0:T(8,128)(2,1)} %get-tuple-element.68), channel_id=1, source_target_pairs={{0,16},{4,20},{8,24},{12,28},{16,0},{20,4},{24,8},{28,12},{1,17},{... | collective-permute-start | bytes 884744 | tf_op jit(solution)/shard_map/ppermute | solution.py:355
  8.4 6.3 %copy-start.28 = (bf16[4,32,1152]{2,1,0:T(8,128)(2,1)S(1)}, bf16[4,32,1152]{2,1,0:T(8,128)(2,1)}, u32[]{:S(2)}) copy-start(bf16[4,32,1152]{2,1,0:T(8,128)(2,1)} %get-tuple-element.71) | copy-start | bytes 884740
  8.4 26.1 %collective-permute-start.11 = (bf16[4,32,1152]{2,1,0:T(8,128)(2,1)}, bf16[4,32,1152]{2,1,0:T(8,128)(2,1)S(1)}, u32[]{:S(2)}, u32[]{:S(2)}) collective-permute-start(bf16[4,32,1152]{2,1,0:T(8,128)(2,1)} %get-tuple-element.69), channel_id=1, source_target_pairs={{0,20},{4,16},{8,28},{12,24},{16,4},{20,0},{24,12},{28,8},{1,21},{... | collective-permute-start | bytes 884744 | tf_op jit(solution)/shard_map/ppermute | solution.py:355
  11.3 30.3 %copy-start.19 = (bf16[4,32,1152]{2,1,0:T(8,128)(2,1)}, bf16[4,32,1152]{2,1,0:T(8,128)(2,1)S(1)}, u32[]{:S(2)}) copy-start(bf16[4,32,1152]{2,1,0:T(8,128)(2,1)S(1)} %collective-permute-done.7.refs_1_) | copy-start | bytes 884740
  11.3 25.2 %collective-permute-start.12 = (bf16[4,32,1152]{2,1,0:T(8,128)(2,1)S(1)}, bf16[4,32,1152]{2,1,0:T(8,128)(2,1)S(1)}, u32[]{:S(2)}, u32[]{:S(2)}) collective-permute-start(bf16[4,32,1152]{2,1,0:T(8,128)(2,1)S(1)} %copy-done.32), channel_id=1, source_target_pairs={{0,24},{4,28},{8,16},{12,20},{16,8},{20,12},{24,0},{28,4},{1,25},{... | collective-permute-start | bytes 884744 | tf_op jit(solution)/shard_map/ppermute | solution.py:355
  14.7 27.0 %copy-start.20 = (bf16[4,32,1152]{2,1,0:T(8,128)(2,1)}, bf16[4,32,1152]{2,1,0:T(8,128)(2,1)S(1)}, u32[]{:S(2)}) copy-start(bf16[4,32,1152]{2,1,0:T(8,128)(2,1)S(1)} %collective-permute-done.8.refs_2_) | copy-start | bytes 884740
  14.7 23.4 %collective-permute-start.13 = (bf16[4,32,1152]{2,1,0:T(8,128)(2,1)S(1)}, bf16[4,32,1152]{2,1,0:T(8,128)(2,1)S(1)}, u32[]{:S(2)}, u32[]{:S(2)}) collective-permute-start(bf16[4,32,1152]{2,1,0:T(8,128)(2,1)S(1)} %copy-done.28), channel_id=1, source_target_pairs={{0,28},{4,24},{8,20},{12,16},{16,12},{20,8},{24,4},{28,0},{1,29},{... | collective-permute-start | bytes 884744 | tf_op jit(solution)/shard_map/ppermute | solution.py:355
  20.6 21.0 %copy-start.21 = (bf16[4,32,1152]{2,1,0:T(8,128)(2,1)}, bf16[4,32,1152]{2,1,0:T(8,128)(2,1)S(1)}, u32[]{:S(2)}) copy-start(bf16[4,32,1152]{2,1,0:T(8,128)(2,1)S(1)} %collective-permute-done.9.refs_3_) | copy-start | bytes 884740
  20.6 17.4 %collective-permute-start = (bf16[4,32,1152]{2,1,0:T(8,128)(2,1)}, bf16[4,32,1152]{2,1,0:T(8,128)(2,1)S(1)}, u32[]{:S(2)}, u32[]{:S(2)}) collective-permute-start(bf16[4,32,1152]{2,1,0:T(8,128)(2,1)} %get-tuple-element.57), channel_id=1, source_target_pairs={{0,4},{4,0},{8,12},{12,8},{16,20},{20,16},{24,28},{28,24},{1,5},{5... | collective-permute-start | bytes 884744 | tf_op jit(solution)/shard_map/ppermute | solution.py:355
  21.1 20.5 %copy-start.22 = (bf16[4,32,1152]{2,1,0:T(8,128)(2,1)}, bf16[4,32,1152]{2,1,0:T(8,128)(2,1)S(1)}, u32[]{:S(2)}) copy-start(bf16[4,32,1152]{2,1,0:T(8,128)(2,1)S(1)} %collective-permute-done.10.refs_4_) | copy-start | bytes 884740
  21.1 18.9 %collective-permute-start.1 = (bf16[4,32,1152]{2,1,0:T(8,128)(2,1)}, bf16[4,32,1152]{2,1,0:T(8,128)(2,1)S(1)}, u32[]{:S(2)}, u32[]{:S(2)}) collective-permute-start(bf16[4,32,1152]{2,1,0:T(8,128)(2,1)} %get-tuple-element.58), channel_id=1, source_target_pairs={{0,8},{4,12},{8,0},{12,4},{16,24},{20,28},{24,16},{28,20},{1,9},{5... | collective-permute-start | bytes 884744 | tf_op jit(solution)/shard_map/ppermute | solution.py:355
  34.5 7.2 %copy-start.24 = (bf16[4,32,1152]{2,1,0:T(8,128)(2,1)}, bf16[4,32,1152]{2,1,0:T(8,128)(2,1)S(1)}, u32[]{:S(2)}) copy-start(bf16[4,32,1152]{2,1,0:T(8,128)(2,1)S(1)} %collective-permute-done.11.refs_5_) | copy-start | bytes 884740
  34.5 25.5 %collective-permute-start.2 = (bf16[4,32,1152]{2,1,0:T(8,128)(2,1)}, bf16[4,32,1152]{2,1,0:T(8,128)(2,1)S(1)}, u32[]{:S(2)}, u32[]{:S(2)}) collective-permute-start(bf16[4,32,1152]{2,1,0:T(8,128)(2,1)} %get-tuple-element.59), channel_id=1, source_target_pairs={{0,12},{4,8},{8,4},{12,0},{16,28},{20,24},{24,20},{28,16},{1,13},{... | collective-permute-start | bytes 884744 | tf_op jit(solution)/shard_map/ppermute | solution.py:355
  36.5 5.1 %copy-start.27 = (bf16[4,32,1152]{2,1,0:T(8,128)(2,1)}, bf16[4,32,1152]{2,1,0:T(8,128)(2,1)S(1)}, u32[]{:S(2)}) copy-start(bf16[4,32,1152]{2,1,0:T(8,128)(2,1)S(1)} %collective-permute-done.12.refs_6_) | copy-start | bytes 884740
  36.5 23.4 %collective-permute-start.3 = (bf16[4,32,1152]{2,1,0:T(8,128)(2,1)}, bf16[4,32,1152]{2,1,0:T(8,128)(2,1)S(1)}, u32[]{:S(2)}, u32[]{:S(2)}) collective-permute-start(bf16[4,32,1152]{2,1,0:T(8,128)(2,1)} %get-tuple-element.60), channel_id=1, source_target_pairs={{0,16},{4,20},{8,24},{12,28},{16,0},{20,4},{24,8},{28,12},{1,17},{... | collective-permute-start | bytes 884744 | tf_op jit(solution)/shard_map/ppermute | solution.py:355
  38.1 3.6 %copy-start.30 = (bf16[4,32,1152]{2,1,0:T(8,128)(2,1)}, bf16[4,32,1152]{2,1,0:T(8,128)(2,1)S(1)}, u32[]{:S(2)}) copy-start(bf16[4,32,1152]{2,1,0:T(8,128)(2,1)S(1)} %collective-permute-done.13.refs_7_) | copy-start | bytes 884740
  38.1 25.5 %collective-permute-start.4 = (bf16[4,32,1152]{2,1,0:T(8,128)(2,1)}, bf16[4,32,1152]{2,1,0:T(8,128)(2,1)S(1)}, u32[]{:S(2)}, u32[]{:S(2)}) collective-permute-start(bf16[4,32,1152]{2,1,0:T(8,128)(2,1)} %get-tuple-element.61), channel_id=1, source_target_pairs={{0,20},{4,16},{8,28},{12,24},{16,4},{20,0},{24,12},{28,8},{1,21},{... | collective-permute-start | bytes 884744 | tf_op jit(solution)/shard_map/ppermute | solution.py:355
  38.1 21.8 %copy-start.23 = (bf16[4,32,1152]{2,1,0:T(8,128)(2,1)}, bf16[4,32,1152]{2,1,0:T(8,128)(2,1)S(1)}, u32[]{:S(2)}) copy-start(bf16[4,32,1152]{2,1,0:T(8,128)(2,1)S(1)} %collective-permute-done.refs_1_) | copy-start | bytes 884740
  38.1 25.5 %collective-permute-start.5 = (bf16[4,32,1152]{2,1,0:T(8,128)(2,1)}, bf16[4,32,1152]{2,1,0:T(8,128)(2,1)S(1)}, u32[]{:S(2)}, u32[]{:S(2)}) collective-permute-start(bf16[4,32,1152]{2,1,0:T(8,128)(2,1)} %get-tuple-element.62), channel_id=1, source_target_pairs={{0,24},{4,28},{8,16},{12,20},{16,8},{20,12},{24,0},{28,4},{1,25},{... | collective-permute-start | bytes 884744 | tf_op jit(solution)/shard_map/ppermute | solution.py:355
  40.0 20.0 %copy-start.25 = (bf16[4,32,1152]{2,1,0:T(8,128)(2,1)}, bf16[4,32,1152]{2,1,0:T(8,128)(2,1)S(1)}, u32[]{:S(2)}) copy-start(bf16[4,32,1152]{2,1,0:T(8,128)(2,1)S(1)} %collective-permute-done.1.refs_2_) | copy-start | bytes 884740
  40.0 23.6 %collective-permute-start.6 = (bf16[4,32,1152]{2,1,0:T(8,128)(2,1)}, bf16[4,32,1152]{2,1,0:T(8,128)(2,1)S(1)}, u32[]{:S(2)}, u32[]{:S(2)}) collective-permute-start(bf16[4,32,1152]{2,1,0:T(8,128)(2,1)} %get-tuple-element.63), channel_id=1, source_target_pairs={{0,28},{4,24},{8,20},{12,16},{16,12},{20,8},{24,4},{28,0},{1,29},{... | collective-permute-start | bytes 884744 | tf_op jit(solution)/shard_map/ppermute | solution.py:355
  60.0 3.6 %copy-start.26 = (bf16[4,32,1152]{2,1,0:T(8,128)(2,1)}, bf16[4,32,1152]{2,1,0:T(8,128)(2,1)S(1)}, u32[]{:S(2)}) copy-start(bf16[4,32,1152]{2,1,0:T(8,128)(2,1)S(1)} %collective-permute-done.2.refs_3_) | copy-start | bytes 884740
  60.0 3.6 %copy-start.29 = (bf16[4,32,1152]{2,1,0:T(8,128)(2,1)}, bf16[4,32,1152]{2,1,0:T(8,128)(2,1)S(1)}, u32[]{:S(2)}) copy-start(bf16[4,32,1152]{2,1,0:T(8,128)(2,1)S(1)} %collective-permute-done.3.refs_4_) | copy-start | bytes 884740
  84.3 3.4 %collective-permute-start.28 = (bf16[4,144,1152]{2,1,0:T(8,128)(2,1)}, bf16[4,144,1152]{2,1,0:T(8,128)(2,1)S(1)}, u32[]{:S(2)}, u32[]{:S(2)}) collective-permute-start(bf16[4,144,1152]{2,1,0:T(8,128)(2,1)} %get-tuple-element.98), channel_id=1, source_target_pairs={{0,4},{4,0},{8,12},{12,8},{16,20},{20,16},{24,28},{28,24},{1,5},{5... | collective-permute-start | bytes 3981320 | tf_op jit(solution)/shard_map/ppermute | solution.py:355
  84.8 10.0 %collective-permute-start.14 = (bf16[4,32,1152]{2,1,0:T(8,128)(2,1)}, bf16[4,32,1152]{2,1,0:T(8,128)(2,1)S(1)}, u32[]{:S(2)}, u32[]{:S(2)}) collective-permute-start(bf16[4,32,1152]{2,1,0:T(8,128)(2,1)} %get-tuple-element.74), channel_id=1, source_target_pairs={{0,4},{4,0},{8,12},{12,8},{16,20},{20,16},{24,28},{28,24},{1,5},{5... | collective-permute-start | bytes 884744 | tf_op jit(solution)/shard_map/ppermute | solution.py:355
  84.9 10.9 %collective-permute-start.15 = (bf16[4,32,1152]{2,1,0:T(8,128)(2,1)}, bf16[4,32,1152]{2,1,0:T(8,128)(2,1)S(1)}, u32[]{:S(2)}, u32[]{:S(2)}) collective-permute-start(bf16[4,32,1152]{2,1,0:T(8,128)(2,1)} %get-tuple-element.75), channel_id=1, source_target_pairs={{0,8},{4,12},{8,0},{12,4},{16,24},{20,28},{24,16},{28,20},{1,9},{5... | collective-permute-start | bytes 884744 | tf_op jit(solution)/shard_map/ppermute | solution.py:355
  85.8 14.4 %collective-permute-start.16 = (bf16[4,32,1152]{2,1,0:T(8,128)(2,1)}, bf16[4,32,1152]{2,1,0:T(8,128)(2,1)S(1)}, u32[]{:S(2)}, u32[]{:S(2)}) collective-permute-start(bf16[4,32,1152]{2,1,0:T(8,128)(2,1)} %get-tuple-element.76), channel_id=1, source_target_pairs={{0,12},{4,8},{8,4},{12,0},{16,28},{20,24},{24,20},{28,16},{1,13},{... | collective-permute-start | bytes 884744 | tf_op jit(solution)/shard_map/ppermute | solution.py:355
  88.8 7.1 %copy-start.31 = (bf16[4,32,1152]{2,1,0:T(8,128)(2,1)S(1)}, bf16[4,32,1152]{2,1,0:T(8,128)(2,1)}, u32[]{:S(2)}) copy-start(bf16[4,32,1152]{2,1,0:T(8,128)(2,1)} %get-tuple-element.77) | copy-start | bytes 884740
  92.3 25.2 %collective-permute-start.29 = (bf16[144,1152]{1,0:T(8,128)(2,1)}, bf16[144,1152]{1,0:T(8,128)(2,1)S(1)}, u32[]{:S(2)}, u32[]{:S(2)}) collective-permute-start(bf16[144,1152]{1,0:T(8,128)(2,1)} %get-tuple-element.100), channel_id=1, source_target_pairs={{0,8},{4,12},{8,0},{12,4},{16,24},{20,28},{24,16},{28,20},{1,9},{5... | collective-permute-start | bytes 995336 | tf_op jit(solution)/shard_map/ppermute | solution.py:355
  93.3 25.5 %collective-permute-start.30 = (bf16[144,1152]{1,0:T(8,128)(2,1)}, bf16[144,1152]{1,0:T(8,128)(2,1)S(1)}, u32[]{:S(2)}, u32[]{:S(2)}) collective-permute-start(bf16[144,1152]{1,0:T(8,128)(2,1)} %get-tuple-element.101), channel_id=1, source_target_pairs={{0,16},{4,20},{8,24},{12,28},{16,0},{20,4},{24,8},{28,12},{1,17},{... | collective-permute-start | bytes 995336 | tf_op jit(solution)/shard_map/ppermute | solution.py:355
  94.8 28.6 %copy-start.1 = (bf16[4,32,1152]{2,1,0:T(8,128)(2,1)}, bf16[4,32,1152]{2,1,0:T(8,128)(2,1)S(1)}, u32[]{:S(2)}) copy-start(bf16[4,32,1152]{2,1,0:T(8,128)(2,1)S(1)} %collective-permute-done.14.refs_1_) | copy-start | bytes 884740
  94.8 24.6 %collective-permute-start.31 = (bf16[144,1152]{1,0:T(8,128)(2,1)}, bf16[144,1152]{1,0:T(8,128)(2,1)S(1)}, u32[]{:S(2)}, u32[]{:S(2)}) collective-permute-start(bf16[144,1152]{1,0:T(8,128)(2,1)} %get-tuple-element.102), channel_id=1, source_target_pairs={{0,24},{4,28},{8,16},{12,20},{16,8},{20,12},{24,0},{28,4},{1,25},{... | collective-permute-start | bytes 995336 | tf_op jit(solution)/shard_map/ppermute | solution.py:355
  95.8 27.6 %copy-start.2 = (bf16[4,32,1152]{2,1,0:T(8,128)(2,1)}, bf16[4,32,1152]{2,1,0:T(8,128)(2,1)S(1)}, u32[]{:S(2)}) copy-start(bf16[4,32,1152]{2,1,0:T(8,128)(2,1)S(1)} %collective-permute-done.15.refs_2_) | copy-start | bytes 884740
  95.8 21.7 %collective-permute-start.17 = (bf16[4,32,1152]{2,1,0:T(8,128)(2,1)S(1)}, bf16[4,32,1152]{2,1,0:T(8,128)(2,1)S(1)}, u32[]{:S(2)}, u32[]{:S(2)}) collective-permute-start(bf16[4,32,1152]{2,1,0:T(8,128)(2,1)S(1)} %copy-done.31), channel_id=1, source_target_pairs={{0,16},{4,20},{8,24},{12,28},{16,0},{20,4},{24,8},{28,12},{1,17},{... | collective-permute-start | bytes 884744 | tf_op jit(solution)/shard_map/ppermute | solution.py:355
  100.2 23.2 %copy-start.3 = (bf16[4,32,1152]{2,1,0:T(8,128)(2,1)}, bf16[4,32,1152]{2,1,0:T(8,128)(2,1)S(1)}, u32[]{:S(2)}) copy-start(bf16[4,32,1152]{2,1,0:T(8,128)(2,1)S(1)} %collective-permute-done.16.refs_3_) | copy-start | bytes 884740
  100.2 23.2 %collective-permute-start.18 = (bf16[4,32,1152]{2,1,0:T(8,128)(2,1)}, bf16[4,32,1152]{2,1,0:T(8,128)(2,1)S(1)}, u32[]{:S(2)}, u32[]{:S(2)}) collective-permute-start(bf16[4,32,1152]{2,1,0:T(8,128)(2,1)} %get-tuple-element.78), channel_id=1, source_target_pairs={{0,20},{4,16},{8,28},{12,24},{16,4},{20,0},{24,12},{28,8},{1,21},{... | collective-permute-start | bytes 884744 | tf_op jit(solution)/shard_map/ppermute | solution.py:355
  117.6 5.9 %copy-start.4 = (bf16[4,32,1152]{2,1,0:T(8,128)(2,1)}, bf16[4,32,1152]{2,1,0:T(8,128)(2,1)S(1)}, u32[]{:S(2)}) copy-start(bf16[4,32,1152]{2,1,0:T(8,128)(2,1)S(1)} %collective-permute-done.17.refs_4_) | copy-start | bytes 884740
  117.6 7.5 %collective-permute-start.21 = (bf16[4,32,1152]{2,1,0:T(8,128)(2,1)}, bf16[4,32,1152]{2,1,0:T(8,128)(2,1)S(1)}, u32[]{:S(2)}, u32[]{:S(2)}) collective-permute-start(bf16[4,32,1152]{2,1,0:T(8,128)(2,1)} %get-tuple-element.82), channel_id=1, source_target_pairs={{0,4},{4,0},{8,12},{12,8},{16,20},{20,16},{24,28},{28,24},{1,5},{5... | collective-permute-start | bytes 884744 | tf_op jit(solution)/shard_map/ppermute | solution.py:355
  117.6 3.4 %copy-start.15 = (bf16[144,1152]{1,0:T(8,128)(2,1)}, bf16[144,1152]{1,0:T(8,128)(2,1)S(1)}, u32[]{:S(2)}) copy-start(bf16[144,1152]{1,0:T(8,128)(2,1)S(1)} %collective-permute-done.29.refs_0_) | copy-start | bytes 995332
  117.6 10.2 %collective-permute-start.22 = (bf16[4,32,1152]{2,1,0:T(8,128)(2,1)}, bf16[4,32,1152]{2,1,0:T(8,128)(2,1)S(1)}, u32[]{:S(2)}, u32[]{:S(2)}) collective-permute-start(bf16[4,32,1152]{2,1,0:T(8,128)(2,1)} %get-tuple-element.83), channel_id=1, source_target_pairs={{0,8},{4,12},{8,0},{12,4},{16,24},{20,28},{24,16},{28,20},{1,9},{5... | collective-permute-start | bytes 884744 | tf_op jit(solution)/shard_map/ppermute | solution.py:355
  118.8 14.2 %collective-permute-start.23 = (bf16[4,32,1152]{2,1,0:T(8,128)(2,1)}, bf16[4,32,1152]{2,1,0:T(8,128)(2,1)S(1)}, u32[]{:S(2)}, u32[]{:S(2)}) collective-permute-start(bf16[4,32,1152]{2,1,0:T(8,128)(2,1)} %get-tuple-element.84), channel_id=1, source_target_pairs={{0,12},{4,8},{8,4},{12,0},{16,28},{20,24},{24,20},{28,16},{1,13},{... | collective-permute-start | bytes 884744 | tf_op jit(solution)/shard_map/ppermute | solution.py:355
  119.4 15.3 %collective-permute-start.24 = (bf16[4,32,1152]{2,1,0:T(8,128)(2,1)}, bf16[4,32,1152]{2,1,0:T(8,128)(2,1)S(1)}, u32[]{:S(2)}, u32[]{:S(2)}) collective-permute-start(bf16[4,32,1152]{2,1,0:T(8,128)(2,1)} %get-tuple-element.85), channel_id=1, source_target_pairs={{0,16},{4,20},{8,24},{12,28},{16,0},{20,4},{24,8},{28,12},{1,17},{... | collective-permute-start | bytes 884744 | tf_op jit(solution)/shard_map/ppermute | solution.py:355
  121.0 14.8 %copy-start.18 = (bf16[4,32,1152]{2,1,0:T(8,128)(2,1)S(1)}, bf16[4,32,1152]{2,1,0:T(8,128)(2,1)}, u32[]{:S(2)}) copy-start(bf16[4,32,1152]{2,1,0:T(8,128)(2,1)} %get-tuple-element.88) | copy-start | bytes 884740
  123.4 18.5 %copy-start.5 = (bf16[4,32,1152]{2,1,0:T(8,128)(2,1)}, bf16[4,32,1152]{2,1,0:T(8,128)(2,1)S(1)}, u32[]{:S(2)}) copy-start(bf16[4,32,1152]{2,1,0:T(8,128)(2,1)S(1)} %collective-permute-done.18.refs_5_) | copy-start | bytes 884740
  123.5 12.4 %collective-permute-start.32 = (bf16[40,1152]{1,0:T(8,128)(2,1)}, bf16[40,1152]{1,0:T(8,128)(2,1)S(1)}, u32[]{:S(2)}, u32[]{:S(2)}) collective-permute-start(bf16[40,1152]{1,0:T(8,128)(2,1)} %get-tuple-element.104), channel_id=1, source_target_pairs={{0,1},{1,0},{2,3},{3,2},{4,5},{5,4},{6,7},{7,6},{8,9},{9,8},{10,11... | collective-permute-start | bytes 276488 | tf_op jit(solution)/shard_map/ppermute | solution.py:355
  125.1 16.8 %copy-start.6 = (bf16[4,32,1152]{2,1,0:T(8,128)(2,1)}, bf16[4,32,1152]{2,1,0:T(8,128)(2,1)S(1)}, u32[]{:S(2)}) copy-start(bf16[4,32,1152]{2,1,0:T(8,128)(2,1)S(1)} %collective-permute-done.21.refs_1_) | copy-start | bytes 884740
  125.1 11.9 %collective-permute-start.33 = (bf16[40,1152]{1,0:T(8,128)(2,1)}, bf16[40,1152]{1,0:T(8,128)(2,1)S(1)}, u32[]{:S(2)}, u32[]{:S(2)}) collective-permute-start(bf16[40,1152]{1,0:T(8,128)(2,1)} %get-tuple-element.105), channel_id=1, source_target_pairs={{0,2},{1,3},{2,0},{3,1},{4,6},{5,7},{6,4},{7,5},{8,10},{9,11},{10,... | collective-permute-start | bytes 276488 | tf_op jit(solution)/shard_map/ppermute | solution.py:355
  127.7 14.2 %copy-start.7 = (bf16[4,32,1152]{2,1,0:T(8,128)(2,1)}, bf16[4,32,1152]{2,1,0:T(8,128)(2,1)S(1)}, u32[]{:S(2)}) copy-start(bf16[4,32,1152]{2,1,0:T(8,128)(2,1)S(1)} %collective-permute-done.22.refs_2_) | copy-start | bytes 884740
  127.7 10.6 %collective-permute-start.34 = (bf16[40,1152]{1,0:T(8,128)(2,1)}, bf16[40,1152]{1,0:T(8,128)(2,1)S(1)}, u32[]{:S(2)}, u32[]{:S(2)}) collective-permute-start(bf16[40,1152]{1,0:T(8,128)(2,1)} %get-tuple-element.106), channel_id=1, source_target_pairs={{0,3},{1,2},{2,1},{3,0},{4,7},{5,6},{6,5},{7,4},{8,11},{9,10},{10,... | collective-permute-start | bytes 276488 | tf_op jit(solution)/shard_map/ppermute | solution.py:355
  133.0 8.9 %copy-start.8 = (bf16[4,32,1152]{2,1,0:T(8,128)(2,1)}, bf16[4,32,1152]{2,1,0:T(8,128)(2,1)S(1)}, u32[]{:S(2)}) copy-start(bf16[4,32,1152]{2,1,0:T(8,128)(2,1)S(1)} %collective-permute-done.23.refs_3_) | copy-start | bytes 884740
  133.0 34.1 %collective-permute-start.25 = (bf16[4,32,1152]{2,1,0:T(8,128)(2,1)}, bf16[4,32,1152]{2,1,0:T(8,128)(2,1)S(1)}, u32[]{:S(2)}, u32[]{:S(2)}) collective-permute-start(bf16[4,32,1152]{2,1,0:T(8,128)(2,1)} %get-tuple-element.86), channel_id=1, source_target_pairs={{0,20},{4,16},{8,28},{12,24},{16,4},{20,0},{24,12},{28,8},{1,21},{... | collective-permute-start | bytes 884744 | tf_op jit(solution)/shard_map/ppermute | solution.py:355
  134.8 7.2 %copy-start.9 = (bf16[4,32,1152]{2,1,0:T(8,128)(2,1)}, bf16[4,32,1152]{2,1,0:T(8,128)(2,1)S(1)}, u32[]{:S(2)}) copy-start(bf16[4,32,1152]{2,1,0:T(8,128)(2,1)S(1)} %collective-permute-done.24.refs_4_) | copy-start | bytes 884740
  134.8 35.9 %collective-permute-start.26 = (bf16[4,32,1152]{2,1,0:T(8,128)(2,1)}, bf16[4,32,1152]{2,1,0:T(8,128)(2,1)S(1)}, u32[]{:S(2)}, u32[]{:S(2)}) collective-permute-start(bf16[4,32,1152]{2,1,0:T(8,128)(2,1)} %get-tuple-element.87), channel_id=1, source_target_pairs={{0,24},{4,28},{8,16},{12,20},{16,8},{20,12},{24,0},{28,4},{1,25},{... | collective-permute-start | bytes 884744 | tf_op jit(solution)/shard_map/ppermute | solution.py:355
  135.8 4.3 %copy-start.38 = (bf16[40,1152]{1,0:T(8,128)(2,1)}, bf16[40,1152]{1,0:T(8,128)(2,1)S(1)}, u32[]{:S(2)}) copy-start(bf16[40,1152]{1,0:T(8,128)(2,1)S(1)} %collective-permute-done.32.refs_0_) | copy-start | bytes 276484
  135.8 34.8 %collective-permute-start.27 = (bf16[4,32,1152]{2,1,0:T(8,128)(2,1)S(1)}, bf16[4,32,1152]{2,1,0:T(8,128)(2,1)S(1)}, u32[]{:S(2)}, u32[]{:S(2)}) collective-permute-start(bf16[4,32,1152]{2,1,0:T(8,128)(2,1)S(1)} %copy-done.18), channel_id=1, source_target_pairs={{0,28},{4,24},{8,20},{12,16},{16,12},{20,8},{24,4},{28,0},{1,29},{... | collective-permute-start | bytes 884744 | tf_op jit(solution)/shard_map/ppermute | solution.py:355
  137.0 37.3 %collective-permute-start.19 = (bf16[4,32,1152]{2,1,0:T(8,128)(2,1)}, bf16[4,32,1152]{2,1,0:T(8,128)(2,1)S(1)}, u32[]{:S(2)}, u32[]{:S(2)}) collective-permute-start(bf16[4,32,1152]{2,1,0:T(8,128)(2,1)} %get-tuple-element.79), channel_id=1, source_target_pairs={{0,24},{4,28},{8,16},{12,20},{16,8},{20,12},{24,0},{28,4},{1,25},{... | collective-permute-start | bytes 884744 | tf_op jit(solution)/shard_map/ppermute | solution.py:355
  138.4 35.9 %collective-permute-start.20 = (bf16[4,32,1152]{2,1,0:T(8,128)(2,1)}, bf16[4,32,1152]{2,1,0:T(8,128)(2,1)S(1)}, u32[]{:S(2)}, u32[]{:S(2)}) collective-permute-start(bf16[4,32,1152]{2,1,0:T(8,128)(2,1)} %get-tuple-element.80), channel_id=1, source_target_pairs={{0,28},{4,24},{8,20},{12,16},{16,12},{20,8},{24,4},{28,0},{1,29},{... | collective-permute-start | bytes 884744 | tf_op jit(solution)/shard_map/ppermute | solution.py:355
  167.1 4.4 %copy-start.10 = (bf16[4,32,1152]{2,1,0:T(8,128)(2,1)}, bf16[4,32,1152]{2,1,0:T(8,128)(2,1)S(1)}, u32[]{:S(2)}) copy-start(bf16[4,32,1152]{2,1,0:T(8,128)(2,1)S(1)} %collective-permute-done.25.refs_5_) | copy-start | bytes 884740
  167.1 10.7 %collective-permute-start.37 = (bf16[40,1152]{1,0:T(8,128)(2,1)}, bf16[40,1152]{1,0:T(8,128)(2,1)S(1)}, u32[]{:S(2)}, u32[]{:S(2)}) collective-permute-start(bf16[40,1152]{1,0:T(8,128)(2,1)} %shard_map.112.refs_0_), channel_id=1, source_target_pairs={{0,3},{1,2},{2,1},{3,0},{4,7},{5,6},{6,5},{7,4},{8,11},{9,10},{10,... | collective-permute-start | bytes 276488 | tf_op jit(solution)/shard_map/ppermute | solution.py:355
  170.7 8.7 %collective-permute-start.36 = (bf16[40,1152]{1,0:T(8,128)(2,1)}, bf16[40,1152]{1,0:T(8,128)(2,1)S(1)}, u32[]{:S(2)}, u32[]{:S(2)}) collective-permute-start(bf16[40,1152]{1,0:T(8,128)(2,1)} %shard_map.112.refs_0_), channel_id=1, source_target_pairs={{0,2},{1,3},{2,0},{3,1},{4,6},{5,7},{6,4},{7,5},{8,10},{9,11},{10,... | collective-permute-start | bytes 276488 | tf_op jit(solution)/shard_map/ppermute | solution.py:355
  170.7 8.6 %collective-permute-start.35 = (bf16[40,1152]{1,0:T(8,128)(2,1)}, bf16[40,1152]{1,0:T(8,128)(2,1)S(1)}, u32[]{:S(2)}, u32[]{:S(2)}) collective-permute-start(bf16[40,1152]{1,0:T(8,128)(2,1)} %shard_map.112.refs_0_), channel_id=1, source_target_pairs={{0,1},{1,0},{2,3},{3,2},{4,5},{5,4},{6,7},{7,6},{8,9},{9,8},{10,11... | collective-permute-start | bytes 276488 | tf_op jit(solution)/shard_map/ppermute | solution.py:355
  (16 other events, 21.2 us)

commit v2 on v1

v2 whole, which is shorter than its diff:
```python
import functools
import math

import jax
import jax.numpy as jnp
from jax import lax
from jax.experimental import pallas as pl
from jax.experimental.pallas import tpu as pltpu
from jax.sharding import PartitionSpec as P


HEADS = 16
LANES = 128
SUB = 16
VMEM = 60 * 1024 * 1024


def dot(a, b, ca, cb):
    return lax.dot_general(a, b, (((ca,), (cb,)), ((), ())), preferred_element_type=jnp.float32)


def pack_kernel(n, clip, low, slots, *refs):
    ntensor, count = 4, len(slots)
    ins, outs = refs[:ntensor], refs[ntensor : ntensor + count]
    buf, sem_in, sem_out = refs[ntensor + count :]
    rank = lax.axis_index("seq")
    part, size = ins[0].shape[2] // n, buf.shape[2]
    reads, writes = [], []
    for j, k in enumerate(slots):
        start = pl.multiple_of((rank ^ k) * part + low, SUB)
        for i, ref in enumerate(ins):
            copy = pltpu.make_async_copy(
                ref.at[clip, 0, pl.ds(start, size), :], buf.at[j, i], sem_in.at[j, i]
            )
            copy.start()
            reads.append(copy)
    for j in range(count):
        for i in range(ntensor):
            reads[j * ntensor + i].wait()
        copy = pltpu.make_async_copy(buf.at[j], outs[j], sem_out.at[j])
        copy.start()
        writes.append(copy)
    for copy in writes:
        copy.wait()


def pack(n, slots, clip, low, size, tensors):
    width, count = tensors[0].shape[3], len(slots)
    block = jax.ShapeDtypeStruct((4, size, width), jnp.bfloat16)
    outs = pl.pallas_call(
        functools.partial(pack_kernel, n, clip, low, slots),
        out_shape=[block] * count,
        in_specs=[pl.BlockSpec(memory_space=pl.ANY)] * 4,
        out_specs=[pl.BlockSpec(memory_space=pl.ANY)] * count,
        scratch_shapes=[
            pltpu.VMEM((count, 4, size, width), jnp.bfloat16),
            pltpu.SemaphoreType.DMA((count, 4)),
            pltpu.SemaphoreType.DMA((count,)),
        ],
        compiler_params=pltpu.CompilerParams(vmem_limit_bytes=VMEM),
        name="pack",
    )(*tensors)
    return dict(zip(slots, outs))


def unpack_kernel(n, clip, low, nprior, *refs):
    ins = refs[:n]
    outs = refs[n + nprior : n + nprior + 4]
    buf, sem_in, sem_out = refs[n + nprior + 4 :]
    rank = lax.axis_index("seq")
    part, size = outs[0].shape[2] // n, buf.shape[2]
    reads, writes = [], []
    for k in range(n):
        copy = pltpu.make_async_copy(ins[k], buf.at[k], sem_in.at[k])
        copy.start()
        reads.append(copy)
    for k in range(n):
        reads[k].wait()
        start = pl.multiple_of((rank ^ k) * part + low, SUB)
        for i, ref in enumerate(outs):
            copy = pltpu.make_async_copy(
                buf.at[k, i], ref.at[clip, 0, pl.ds(start, size), :], sem_out.at[k, i]
            )
            copy.start()
            writes.append(copy)
    for copy in writes:
        copy.wait()


def unpack(n, clip, low, full, blocks, prior):
    part, width = blocks[0].shape[1:]
    nprior = len(prior)
    return pl.pallas_call(
        functools.partial(unpack_kernel, n, clip, low, nprior),
        out_shape=[jax.ShapeDtypeStruct(full, jnp.bfloat16)] * 4,
        in_specs=[pl.BlockSpec(memory_space=pl.ANY)] * (n + nprior),
        out_specs=[pl.BlockSpec(memory_space=pl.ANY)] * 4,
        input_output_aliases={n + i: i for i in range(nprior)},
        scratch_shapes=[
            pltpu.VMEM((n, 4, part, width), jnp.bfloat16),
            pltpu.SemaphoreType.DMA((n,)),
            pltpu.SemaphoreType.DMA((n, 4)),
        ],
        compiler_params=pltpu.CompilerParams(vmem_limit_bytes=VMEM),
        name="unpack",
    )(*blocks, *prior)


def attend_kernel(n, clip, low, share, last, nprior, frames_ref, places_ref, *refs):
    ins, weight_ref = refs[:n], refs[n]
    prior, refs = refs[n + 1 : n + 1 + nprior], refs[n + 1 + nprior :]
    outs, refs = refs[:n], refs[n:]
    extra, refs = refs[: 1 + last], refs[1 + last :]
    x_s, y_s, c_s, o_s, w_s, gw_s, sem_in, sem_w, sem_out, sem_gw = refs
    rank = lax.axis_index("seq")
    part, width = ins[0].shape[1:]
    nblock = part // SUB
    rows = n * SUB
    every = n * part
    head_dim = width // HEADS
    inv_root = 1.0 / math.sqrt(head_dim)
    nframe_live = frames_ref[clip]
    nplace_live = places_ref[clip] - (rank * share + low)

    reads = [pltpu.make_async_copy(weight_ref, w_s, sem_w.at[0])]
    reads += [pltpu.make_async_copy(ins[k], x_s.at[k], sem_in.at[k]) for k in range(n)]
    prior_reads = [pltpu.make_async_copy(ref, gw_s, sem_w.at[1]) for ref in prior]
    for copy in reads:
        copy.start()

    def frame(row):
        return (row // part) ^ rank

    row_id = lax.broadcasted_iota(jnp.int32, (every, 1), 0)
    alive = (frame(row_id) < nframe_live) & (row_id % part < nplace_live)
    key_id = lax.broadcasted_iota(jnp.int32, (rows, 1), 0)
    query_id = lax.broadcasted_iota(jnp.int32, (1, rows), 1)
    key_alive = ((key_id // SUB) ^ rank) < nframe_live
    allowed = ((key_id % SUB) == (query_id % SUB)) & key_alive
    block_alive = ((key_id // SUB) ^ rank) < nframe_live

    for copy in reads:
        copy.wait()
    for copy in prior_reads:
        copy.start()
    grad = x_s[:, 3].reshape(every, width)
    cot = jnp.where(alive, dot(grad, w_s[...], 1, 0), 0.0).astype(jnp.bfloat16)
    c_s[...] = cot.reshape(n, part, width)

    window_lane = lax.broadcasted_iota(jnp.int32, (1, 2 * LANES), 1)

    def pairs(b, carry):
        these = pl.ds(pl.multiple_of(b * SUB, SUB), SUB)
        live = block_alive & (b * SUB + key_id % SUB < nplace_live)
        for j in range(HEADS // 2):
            lanes = slice(j * LANES, (j + 2) * LANES)
            first = 2 * head_dim * j - LANES * j
            own = [
                (window_lane >= first + h * head_dim) & (window_lane < first + (h + 1) * head_dim)
                for h in range(2)
            ]

            def both(x):
                zero = jnp.zeros_like(x)
                return jnp.concatenate([jnp.where(m, x, zero) for m in own], axis=0)

            qw, kw, vw = (x_s[:, i, these, lanes].reshape(rows, 2 * LANES) for i in range(3))
            cw = c_s[:, these, lanes].reshape(rows, 2 * LANES)
            q2, k2, v2, c2 = both(qw), both(kw), both(vw), both(cw)
            scores = dot(k2, qw, 1, 1)
            gattns = dot(v2, cw, 1, 1)
            rounded, high, low = [], [], []
            for h in range(2):
                part_of = slice(h * rows, (h + 1) * rows)
                score = jnp.where(allowed, scores[part_of] * inv_root, -1e30)
                expo = jnp.exp(score - jnp.max(score, axis=0, keepdims=True))
                weights = expo * (1.0 / jnp.sum(expo, axis=0, keepdims=True))
                rounded.append(weights.astype(jnp.bfloat16))
                gattn = gattns[part_of]
                delta = jnp.sum(weights * gattn, axis=0, keepdims=True)
                gscore = weights * ((gattn - delta) * inv_root)
                high.append(gscore.astype(jnp.bfloat16))
                low.append((gscore - high[h].astype(jnp.float32)).astype(jnp.bfloat16))
            across = [jnp.concatenate(x, axis=1) for x in (rounded, high, low)]
            down = [jnp.concatenate(x, axis=0) for x in (rounded, high, low)]
            out = jnp.where(live, dot(down[0], v2, 0, 0), 0.0)
            dq = dot(down[1], k2, 0, 0) + dot(down[2], k2, 0, 0)
            dv = dot(across[0], c2, 1, 0)
            dk = dot(across[1], q2, 1, 0) + dot(across[2], q2, 1, 0)
            mine = window_lane[:, :LANES] >= first
            lead = slice(j * LANES, (j + 1) * LANES)
            tail = slice((j + 1) * LANES, (j + 2) * LANES)
            targets = [o_s] + [y_s.at[:, i] for i in (1, 2, 3)]
            for ref, value in zip(targets, (out, dq, dk, dv)):
                value = value.astype(jnp.bfloat16).reshape(n, SUB, 2 * LANES)
                if j:
                    ref[:, these, lead] = jnp.where(mine[None], value[:, :, :LANES], ref[:, these, lead])
                else:
                    ref[:, these, lead] = value[:, :, :LANES]
                ref[:, these, tail] = value[:, :, LANES:]
        return carry

    lax.fori_loop(0, nblock, pairs, 0)

    writes = []

    def send(source, target, sem):
        copy = pltpu.make_async_copy(source, target, sem)
        copy.start()
        writes.append(copy)

    for k in range(n):
        send(y_s.at[k, pl.ds(1, 3)], outs[k].at[pl.ds(1, 3)], sem_out.at[1, k])
    for copy in prior_reads:
        copy.wait()
    tile = width // 3
    for i in range(3):
        cols = slice(i * tile, (i + 1) * tile)
        total = dot(x_s[:, 3, :, cols].reshape(every, tile), o_s[...].reshape(every, width), 0, 0)
        gw_s[cols, :] = gw_s[cols, :] + total if nprior else total
    if last:
        half, count = n // 2, width // n
        give, keep = extra
        core = rank % 2
        for m in range(half):
            here = pl.multiple_of((2 * m + core) * count, 8)
            keep[m] = gw_s[pl.ds(here, count), :].astype(jnp.bfloat16)
            there = pl.multiple_of((2 * m + 1 - core) * count, 8)
            give[m] = gw_s[pl.ds(there, count), :].astype(jnp.bfloat16)
    else:
        send(gw_s, extra[0], sem_gw.at[0])
    projected = dot(o_s[...].reshape(every, width), w_s[...], 1, 1).astype(jnp.bfloat16)
    y_s[:, 0] = projected.reshape(n, part, width)
    for k in range(n):
        send(y_s.at[k, 0], outs[k].at[0], sem_out.at[0, k])
    for copy in writes:
        copy.wait()


def attend(n, clip, low, share, last, frame_count, pos_count, blocks, weight, prior):
    part, width = blocks[0].shape[1:]
    vmem = pl.BlockSpec(memory_space=pltpu.VMEM)
    smem = pl.BlockSpec(memory_space=pltpu.SMEM)
    hbm = pl.BlockSpec(memory_space=pl.ANY)
    nprior = len(prior)
    block = jax.ShapeDtypeStruct((4, part, width), jnp.bfloat16)
    if last:
        halves = (n // 2, width // n, width)
        extra = [jax.ShapeDtypeStruct(halves, jnp.bfloat16)] * 2
        espec = [vmem, vmem]
    else:
        extra, espec = [jax.ShapeDtypeStruct((width, width), jnp.float32)], [hbm]
    return pl.pallas_call(
        functools.partial(attend_kernel, n, clip, low, share, last, nprior),
        out_shape=[block] * n + extra,
        in_specs=[smem, smem] + [hbm] * (n + 1 + nprior),
        out_specs=[hbm] * n + espec,
        scratch_shapes=[
            pltpu.VMEM((n, 4, part, width), jnp.bfloat16),
            pltpu.VMEM((n, 4, part, width), jnp.bfloat16),
            pltpu.VMEM((n, part, width), jnp.bfloat16),
            pltpu.VMEM((n, part, width), jnp.bfloat16),
            pltpu.VMEM((width, width), jnp.bfloat16),
            pltpu.VMEM((width, width), jnp.float32),
            pltpu.SemaphoreType.DMA((n,)),
            pltpu.SemaphoreType.DMA((2,)),
            pltpu.SemaphoreType.DMA((2, n)),
            pltpu.SemaphoreType.DMA((n // 2,)),
        ],
        compiler_params=pltpu.CompilerParams(vmem_limit_bytes=VMEM),
        cost_estimate=pl.CostEstimate(
            flops=10_000_000_000, bytes_accessed=16_000_000, transcendentals=0
        ),
        name="attend",
    )(frame_count, pos_count, *blocks, weight, *prior)


def small_call(kernel, out_shape, args, scratch=()):
    vmem = pl.BlockSpec(memory_space=pltpu.VMEM)
    return pl.pallas_call(
        kernel,
        out_shape=out_shape,
        in_specs=[vmem] * len(args),
        out_specs=[vmem] * len(out_shape),
        scratch_shapes=list(scratch),
        compiler_params=pltpu.CompilerParams(vmem_limit_bytes=VMEM),
        cost_estimate=pl.CostEstimate(
            flops=1_000_000_000, bytes_accessed=4_000_000, transcendentals=0
        ),
    )(*args)


def chip_sum_kernel(half, keep, came, own, *outs):
    chip = lax.axis_index("seq") // 2
    own[...] = keep[chip].astype(jnp.float32) + came[chip].astype(jnp.float32)
    for q in range(1, half):
        total = keep[chip ^ q].astype(jnp.float32) + came[chip ^ q].astype(jnp.float32)
        outs[q - 1][...] = total.astype(jnp.bfloat16)


def plane_sum_kernel(half, nrep, own, *refs):
    came, mine, outs, acc = refs[: half - 1], refs[half - 1], refs[half:-1], refs[-1]
    plane = lax.axis_index("rep")
    count, share = own.shape[0], mine.shape[0]
    acc[...] = jnp.zeros_like(acc)
    total = own[...]
    for ref in came:
        total = total + ref[...].astype(jnp.float32)
    acc[:count, :] = total
    mine[...] = acc[pl.ds(pl.multiple_of(plane * share, 8), share), :]
    for w in range(1, nrep):
        there = pl.multiple_of((plane ^ w) * share, 8)
        outs[w - 1][...] = acc[pl.ds(there, share), :].astype(jnp.bfloat16)


def replica_sum_kernel(mine, *refs):
    total = mine[...]
    for ref in refs[:-1]:
        total = total + ref[...].astype(jnp.float32)
    refs[-1][...] = total.astype(jnp.bfloat16)


def assemble_kernel(nrep, *refs):
    parts, out, acc = refs[:nrep], refs[-2], refs[-1]
    plane = lax.axis_index("rep")
    share = parts[0].shape[0]
    for w in range(nrep):
        there = pl.multiple_of((plane ^ w) * share, 8)
        acc[pl.ds(there, share), :] = parts[w][...].astype(jnp.float32)
    out[...] = acc[: out.shape[0], :]


def permute(x, axis, size, step):
    return lax.ppermute(x, axis, [(i, i ^ step) for i in range(size)])


def exchange(n, order, blocks):
    moved = [None] * n
    moved[0] = blocks[0]
    for k in order:
        moved[k] = permute(blocks[k], "seq", n, k)
    return moved


def reduce_weight(n, nrep, give, keep):
    half, count, width = keep.shape
    came = permute(give, "seq", n, 1)
    wide = jax.ShapeDtypeStruct((count, width), jnp.float32)
    narrow = jax.ShapeDtypeStruct((count, width), jnp.bfloat16)
    own, *sends = small_call(
        functools.partial(chip_sum_kernel, half), [wide] + [narrow] * (half - 1), [keep, came]
    )
    came = [permute(sends[q - 1], "seq", n, 2 * q) for q in range(1, half)]
    share = -(-(-(-count // nrep)) // 8) * 8
    acc = pltpu.VMEM((nrep * share, width), jnp.float32)
    wide = jax.ShapeDtypeStruct((share, width), jnp.float32)
    narrow = jax.ShapeDtypeStruct((share, width), jnp.bfloat16)
    mine, *sends = small_call(
        functools.partial(plane_sum_kernel, half, nrep),
        [wide] + [narrow] * (nrep - 1),
        [own, *came],
        [acc],
    )
    came = [permute(sends[w - 1], "rep", nrep, w) for w in range(1, nrep)]
    (mine,) = small_call(replica_sum_kernel, [narrow], [mine, *came])
    came = [permute(mine, "rep", nrep, w) for w in range(1, nrep)]
    (out,) = small_call(
        functools.partial(assemble_kernel, nrep),
        [jax.ShapeDtypeStruct((count, width), jnp.float32)],
        [mine, *came],
        [acc],
    )
    return out


def send_order(n):
    return sorted(range(1, n), key=lambda k: (k < 2, -bin(k >> 1).count("1"), k))


def plan(nclip, share):
    return [(c, 0, share) for c in range(nclip)]


def shards(n, nrep, query_rows, key_rows, value_rows, out_grad, out_weight, frame_count, pos_count):
    nclip, frame_local, npos, _ = query_rows.shape
    if frame_local != 1 or n & (n - 1) or nrep & (nrep - 1) or (npos // n) % SUB:
        raise ValueError("sizes")
    order = send_order(n)
    tensors = (query_rows, key_rows, value_rows, out_grad)
    share = npos // n
    chunks = plan(nclip, share)
    arrived = []
    for chunk in chunks:
        blocks = {}
        for slots in (order[:2], order[2:] + [0]):
            blocks.update(pack(n, slots, *chunk, tensors))
        arrived.append(exchange(n, order, blocks))
    extra, back = (), []
    for c, (clip, low, _) in enumerate(chunks):
        last = c == len(chunks) - 1
        done = attend(
            n, clip, low, share, last, frame_count, pos_count, arrived[c], out_weight, extra
        )
        blocks, extra = done[:n], done[n:]
        back.append(exchange(n, order, blocks))
    wgrad = reduce_weight(n, nrep, *extra)
    outs = ()
    for c, (clip, low, _) in enumerate(chunks):
        outs = unpack(n, clip, low, query_rows.shape, back[c], outs)
    return (*outs, wgrad)


def solution(mesh):
    n, nrep = mesh.shape["seq"], mesh.shape["rep"]
    rows = P("rep", "seq", None, None)
    return jax.shard_map(
        functools.partial(shards, n, nrep),
        mesh=mesh,
        in_specs=(rows, rows, rows, rows, P(), P("rep"), P("rep")),
        out_specs=(rows, rows, rows, rows, P("seq", None)),
        check_vma=False,
    )
```

time: 183 us -> 180 us (0.984)
  Pallas kernels: 58.9 us -> 54.6 us
  starting transfers between devices: 51.1 us -> 49.2 us
    pallas_call x6 -> x8, Pallas kernels: 49.2 us -> 45.4 us  [the longest x2 31 us: attend(): pl.pallas_call(functools.partial(attend_kernel, n, clip, low, share, last...]
    ppermute x38, starting transfers between devices: 51.1 us -> 49.2 us  [permute(): return lax.ppermute(x, axis, [(i, i ^ step) for i in range(size)])]
    ppermute x38, waiting for transfers between devices: 67.4 us -> 69.2 us  [permute(): return lax.ppermute(x, axis, [(i, i ^ step) for i in range(size)])]
    unnamed x84 -> x80, local copies, waits for them, and re-layouts: 4.21 us -> 4.98 us
  transfers between devices with their start and end apart: 38 -> 38, of which waited for: 12 -> 13; matrix products, arithmetic and copies ran while one was open for 0% -> 0% of each run, Pallas kernels for 19% -> 19%
where the time goes in v2:
time: 180 us; the launch traced here: 179 us
  waiting for transfers between devices  69.2 us (38%)
  Pallas kernels  54.6 us (30%)
  starting transfers between devices  49.2 us (27%)
  local copies, waits for them, and re-layouts  4.98 us (3%)
    ppermute x38, waiting for transfers between devices, permute(): return lax.ppermute(x, axis, [(i, i ^ step) for i in range(size)])  69.2 us
    ppermute x38, starting transfers between devices, permute(): return lax.ppermute(x, axis, [(i, i ^ step) for i in range(size)])  49.2 us
    pallas_call x2, Pallas kernels, attend(): pl.pallas_call(functools.partial(attend_kernel, n, clip, low, share, last...  31 us
    pallas_call x4, Pallas kernels, small_call(): pl.pallas_call(kernel, out_shape=out_shape, in_specs=[vmem] * len(args),...  9.18 us
    pallas_call x4, Pallas kernels, pack(): pl.pallas_call(functools.partial(pack_kernel, n, clip, low, slots), out_s...  8.95 us
    pallas_call x2, Pallas kernels, unpack(): pl.pallas_call(functools.partial(unpack_kernel, n, clip, low, nprior), ou...  5.4 us
    unnamed x80, local copies, waits for them, and re-layouts  4.98 us
  transfers between devices with their start and end apart: 38, of which 13 were waited for; matrix products, arithmetic and copies ran while one was open for 0% of the time, Pallas kernels for 19%

profile of v2, /device:TPU:0, one launch (start us, length us, event | category | flops | bytes accessed | tf_op | source)
XLA Modules:
  0.0 179.0 jit_solution(4215308332165573506)
XLA Ops:
  0.6 1.9 %pack.5 = (bf16[4,32,1152]{2,1,0:T(8,128)(2,1)}, bf16[4,32,1152]{2,1,0:T(8,128)(2,1)}) custom-call(bf16[2,1,256,1152]{3,2,1,0:T(8,128)(2,1)} %refs_0_.7, bf16[2,1,256,1152]{3,2,1,0:T(8,128)(2,1)} %refs_1_.7, bf16[2,1,256,1152]{3,2,1,0:T(8,128)(2,1)} %refs_2_.7, bf16[2,1,256,1152]{3,2,1,0:T(8,128)(2,1)} %refs_3_.7), custom_call_target="tpu_custom_call" | custom-call | tf_op jit(solution)/shard_map/pack/pallas_call | solution.py:50
  2.6 4.0 %collective-permute-start.5 = (bf16[4,32,1152]{2,1,0:T(8,128)(2,1)}, bf16[4,32,1152]{2,1,0:T(8,128)(2,1)S(1)}, u32[]{:S(2)}, u32[]{:S(2)}) collective-permute-start(bf16[4,32,1152]{2,1,0:T(8,128)(2,1)} %get-tuple-element.62), channel_id=1, source_target_pairs={{0,24},{4,28},{8,16},{12,20},{16,8},{20,12},{24,0},{28,4},{1,25},{... | collective-permute-start | bytes 884744 | tf_op jit(solution)/shard_map/ppermute | solution.py:334
  6.6 1.9 %pack.7 = (bf16[4,32,1152]{2,1,0:T(8,128)(2,1)}, bf16[4,32,1152]{2,1,0:T(8,128)(2,1)}) custom-call(bf16[2,1,256,1152]{3,2,1,0:T(8,128)(2,1)} %refs_0_.7, bf16[2,1,256,1152]{3,2,1,0:T(8,128)(2,1)} %refs_1_.7, bf16[2,1,256,1152]{3,2,1,0:T(8,128)(2,1)} %refs_2_.7, bf16[2,1,256,1152]{3,2,1,0:T(8,128)(2,1)} %refs_3_.7), custom_call_target="tpu_custom_call" | custom-call | tf_op jit(solution)/shard_map/pack/pallas_call | solution.py:50
  8.5 2.1 %collective-permute-start.12 = (bf16[4,32,1152]{2,1,0:T(8,128)(2,1)}, bf16[4,32,1152]{2,1,0:T(8,128)(2,1)S(1)}, u32[]{:S(2)}, u32[]{:S(2)}) collective-permute-start(bf16[4,32,1152]{2,1,0:T(8,128)(2,1)} %get-tuple-element.70), channel_id=1, source_target_pairs={{0,24},{4,28},{8,16},{12,20},{16,8},{20,12},{24,0},{28,4},{1,25},{... | collective-permute-start | bytes 884744 | tf_op jit(solution)/shard_map/ppermute | solution.py:334
  10.7 0.6 collective-permute-start.13
  11.3 2.5 %pack.6 = (bf16[4,32,1152]{2,1,0:T(8,128)(2,1)}, bf16[4,32,1152]{2,1,0:T(8,128)(2,1)}, bf16[4,32,1152]{2,1,0:T(8,128)(2,1)}, bf16[4,32,1152]{2,1,0:T(8,128)(2,1)...) custom-call(bf16[2,1,256,1152]{3,2,1,0:T(8,128)(2,1)} %refs_0_.7, bf16[2,1,256,1152]{3,2,1,0:T(8,128)(2,1)} %refs_1_.7, ...), custom_call_target="tpu_custom_call" | custom-call | tf_op jit(solution)/shard_map/pack/pallas_call | solution.py:50
  13.8 0.4 collective-permute-start.7
  14.2 0.4 collective-permute-done.5.refs_6_
  14.6 2.0 %collective-permute-start.8 = (bf16[4,32,1152]{2,1,0:T(8,128)(2,1)}, bf16[4,32,1152]{2,1,0:T(8,128)(2,1)S(1)}, u32[]{:S(2)}, u32[]{:S(2)}) collective-permute-start(bf16[4,32,1152]{2,1,0:T(8,128)(2,1)} %get-tuple-element.66), channel_id=1, source_target_pairs={{0,8},{4,12},{8,0},{12,4},{16,24},{20,28},{24,16},{28,20},{1,9},{5... | collective-permute-start | bytes 884744 | tf_op jit(solution)/shard_map/ppermute | solution.py:334
  16.6 4.0 %collective-permute-done.6.refs_7_ = bf16[4,32,1152]{2,1,0:T(8,128)(2,1)S(1)} collective-permute-done((bf16[4,32,1152]{2,1,0:T(8,128)(2,1)}, bf16[4,32,1152]{2,1,0:T(8,128)(2,1)S(1)}, u32[]{:S(2)}, u32[]{:S(2)}) %collective-permute-start.6) | collective-permute-done | bytes 294944 | tf_op jit(solution)/shard_map/ppermute | solution.py:334
  20.6 1.7 collective-permute-start.9
  22.4 4.9 %collective-permute-done.12.refs_6_ = bf16[4,32,1152]{2,1,0:T(8,128)(2,1)S(1)} collective-permute-done((bf16[4,32,1152]{2,1,0:T(8,128)(2,1)}, bf16[4,32,1152]{2,1,0:T(8,128)(2,1)S(1)}, u32[]{:S(2)}, u32[]{:S(2)}) %collective-permute-start.12) | collective-permute-done | bytes 294944 | tf_op jit(solution)/shard_map/ppermute | solution.py:334
  27.3 2.0 %collective-permute-start.10 = (bf16[4,32,1152]{2,1,0:T(8,128)(2,1)}, bf16[4,32,1152]{2,1,0:T(8,128)(2,1)S(1)}, u32[]{:S(2)}, u32[]{:S(2)}) collective-permute-start(bf16[4,32,1152]{2,1,0:T(8,128)(2,1)} %get-tuple-element.68), channel_id=1, source_target_pairs={{0,16},{4,20},{8,24},{12,28},{16,0},{20,4},{24,8},{28,12},{1,17},{... | collective-permute-start | bytes 884744 | tf_op jit(solution)/shard_map/ppermute | solution.py:334
  29.3 4.0 %collective-permute-done.13.refs_7_ = bf16[4,32,1152]{2,1,0:T(8,128)(2,1)S(1)} collective-permute-done((bf16[4,32,1152]{2,1,0:T(8,128)(2,1)}, bf16[4,32,1152]{2,1,0:T(8,128)(2,1)S(1)}, u32[]{:S(2)}, u32[]{:S(2)}) %collective-permute-start.13) | collective-permute-done | bytes 294944 | tf_op jit(solution)/shard_map/ppermute | solution.py:334
  33.3 1.8 collective-permute-start.11
  35.1 2.5 %pack.4 = (bf16[4,32,1152]{2,1,0:T(8,128)(2,1)}, bf16[4,32,1152]{2,1,0:T(8,128)(2,1)}, bf16[4,32,1152]{2,1,0:T(8,128)(2,1)}, bf16[4,32,1152]{2,1,0:T(8,128)(2,1)...) custom-call(bf16[2,1,256,1152]{3,2,1,0:T(8,128)(2,1)} %refs_0_.7, bf16[2,1,256,1152]{3,2,1,0:T(8,128)(2,1)} %refs_1_.7, ...), custom_call_target="tpu_custom_call" | custom-call | tf_op jit(solution)/shard_map/pack/pallas_call | solution.py:50
  37.7 2.7 %collective-permute-done.8.refs_2_ = bf16[4,32,1152]{2,1,0:T(8,128)(2,1)S(1)} collective-permute-done((bf16[4,32,1152]{2,1,0:T(8,128)(2,1)}, bf16[4,32,1152]{2,1,0:T(8,128)(2,1)S(1)}, u32[]{:S(2)}, u32[]{:S(2)}) %collective-permute-start.8) | collective-permute-done | bytes 294944 | tf_op jit(solution)/shard_map/ppermute | solution.py:334
  40.5 1.5 collective-permute-start.1
  42.0 3.9 %collective-permute-done.9.refs_3_ = bf16[4,32,1152]{2,1,0:T(8,128)(2,1)S(1)} collective-permute-done((bf16[4,32,1152]{2,1,0:T(8,128)(2,1)}, bf16[4,32,1152]{2,1,0:T(8,128)(2,1)S(1)}, u32[]{:S(2)}, u32[]{:S(2)}) %collective-permute-start.9) | collective-permute-done | bytes 294944 | tf_op jit(solution)/shard_map/ppermute | solution.py:334
  45.9 1.8 %collective-permute-start.2 = (bf16[4,32,1152]{2,1,0:T(8,128)(2,1)}, bf16[4,32,1152]{2,1,0:T(8,128)(2,1)S(1)}, u32[]{:S(2)}, u32[]{:S(2)}) collective-permute-start(bf16[4,32,1152]{2,1,0:T(8,128)(2,1)} %get-tuple-element.59), channel_id=1, source_target_pairs={{0,12},{4,8},{8,4},{12,0},{16,28},{20,24},{24,20},{28,16},{1,13},{... | collective-permute-start | bytes 884744 | tf_op jit(solution)/shard_map/ppermute | solution.py:334
  47.7 0.5 collective-permute-start.3
  48.3 0.2 copy-done.29
  48.4 0.5 copy-done.31
  49.0 14.6 %attend.2 = (bf16[4,32,1152]{2,1,0:T(8,128)(2,1)}, bf16[4,32,1152]{2,1,0:T(8,128)(2,1)}, bf16[4,32,1152]{2,1,0:T(8,128)(2,1)}, bf16[4,32,1152]{2,1,0:T(8,128)(2,...) custom-call(s32[2]{0:T(128)} %frames_ref.3, ...), custom_call_target="tpu_custom_call" | custom-call | flops 10000000000 | bytes 16000000 | tf_op jit(solution)/shard_map/attend/pallas_call | solution.py:253
  63.7 0.6 copy-done.25
  64.7 16.4 %attend.3 = (bf16[4,32,1152]{2,1,0:T(8,128)(2,1)}, bf16[4,32,1152]{2,1,0:T(8,128)(2,1)}, bf16[4,32,1152]{2,1,0:T(8,128)(2,1)}, bf16[4,32,1152]{2,1,0:T(8,128)(2,...) custom-call(s32[2]{0:T(128)} %frames_ref.3, ...), custom_call_target="tpu_custom_call" | custom-call | flops 10000000000 | bytes 16000000 | tf_op jit(solution)/shard_map/attend/pallas_call | solution.py:253
  81.1 1.0 collective-permute-start.28
  82.2 0.5 collective-permute-start.15
  82.8 1.3 collective-permute-start.16
  84.0 1.0 collective-permute-done.28.came
  85.1 1.1 copy-done.14
  86.1 3.1 %shard_map.110 = (f32[144,1152]{1,0:T(8,128)}, bf16[144,1152]{1,0:T(8,128)(2,1)}, bf16[144,1152]{1,0:T(8,128)(2,1)}, bf16[144,1152]{1,0:T(8,128)(2,1)}) custom-call(bf16[4,144,1152]{2,1,0:T(8,128)(2,1)} %get-tuple-element.97.keep, bf16[4,144,1152]{2,1,0:T(8,128)(2,1)} %copy-done.14), custom_call_target="tpu_custom_call" | custom-call | flops 1000000000 | bytes 4000000 | tf_op jit(solution)/shard_map/pallas_call | solution.py:280
  89.2 0.5 collective-permute-start.29
  89.7 0.9 collective-permute-start.30
  90.7 2.0 %collective-permute-start.31 = (bf16[144,1152]{1,0:T(8,128)(2,1)}, bf16[144,1152]{1,0:T(8,128)(2,1)S(1)}, u32[]{:S(2)}, u32[]{:S(2)}) collective-permute-start(bf16[144,1152]{1,0:T(8,128)(2,1)} %get-tuple-element.102), channel_id=1, source_target_pairs={{0,24},{4,28},{8,16},{12,20},{16,8},{20,12},{24,0},{28,4},{1,25},{... | collective-permute-start | bytes 995336 | tf_op jit(solution)/shard_map/ppermute | solution.py:334
  92.7 1.0 collective-permute-start.17
  93.7 3.9 %collective-permute-done.16.refs_3_ = bf16[4,32,1152]{2,1,0:T(8,128)(2,1)S(1)} collective-permute-done((bf16[4,32,1152]{2,1,0:T(8,128)(2,1)}, bf16[4,32,1152]{2,1,0:T(8,128)(2,1)S(1)}, u32[]{:S(2)}, u32[]{:S(2)}) %collective-permute-start.16) | collective-permute-done | bytes 294944 | tf_op jit(solution)/shard_map/ppermute | solution.py:334
  97.6 1.8 collective-permute-start.18
  99.4 14.7 %collective-permute-done.17.refs_4_ = bf16[4,32,1152]{2,1,0:T(8,128)(2,1)S(1)} collective-permute-done((bf16[4,32,1152]{2,1,0:T(8,128)(2,1)S(1)}, bf16[4,32,1152]{2,1,0:T(8,128)(2,1)S(1)}, u32[]{:S(2)}, u32[]{:S(2)}) %collective-permute-start.17) | collective-permute-done | bytes 294944 | tf_op jit(solution)/shard_map/ppermute | solution.py:334
  114.1 1.6 collective-permute-start.22
  115.6 0.3 collective-permute-start.23
  115.9 0.9 collective-permute-start.24
  116.9 2.4 %shard_map.111 = (f32[40,1152]{1,0:T(8,128)}, bf16[40,1152]{1,0:T(8,128)(2,1)}, bf16[40,1152]{1,0:T(8,128)(2,1)}, bf16[40,1152]{1,0:T(8,128)(2,1)}) custom-call(f32[144,1152]{1,0:T(8,128)} %get-tuple-element.99.own, bf16[144,1152]{1,0:T(8,128)(2,1)} %copy-done.15, bf16[144,1152]{1,0:T(8,128)(2,1)} %copy-done.16, bf16[144,1152]{1,0:T(8,128)(2,1)} %copy-done.17), custom_call_target="tpu_custom_call" | custom-call | flops 1000000000 | bytes 4000000 | tf_op jit(solution)/shard_map/pallas_call | solution.py:280
  119.3 1.6 collective-permute-start.32
  121.0 2.6 %collective-permute-start.33 = (bf16[40,1152]{1,0:T(8,128)(2,1)}, bf16[40,1152]{1,0:T(8,128)(2,1)S(1)}, u32[]{:S(2)}, u32[]{:S(2)}) collective-permute-start(bf16[40,1152]{1,0:T(8,128)(2,1)} %get-tuple-element.105), channel_id=1, source_target_pairs={{0,2},{1,3},{2,0},{3,1},{4,6},{5,7},{6,4},{7,5},{8,10},{9,11},{10,... | collective-permute-start | bytes 276488 | tf_op jit(solution)/shard_map/ppermute | solution.py:334
  123.6 0.7 collective-permute-done.22.refs_2_
  124.2 3.6 %collective-permute-start.34 = (bf16[40,1152]{1,0:T(8,128)(2,1)}, bf16[40,1152]{1,0:T(8,128)(2,1)S(1)}, u32[]{:S(2)}, u32[]{:S(2)}) collective-permute-start(bf16[40,1152]{1,0:T(8,128)(2,1)} %get-tuple-element.106), channel_id=1, source_target_pairs={{0,3},{1,2},{2,1},{3,0},{4,7},{5,6},{6,5},{7,4},{8,11},{9,10},{10,... | collective-permute-start | bytes 276488 | tf_op jit(solution)/shard_map/ppermute | solution.py:334
  127.8 1.6 collective-permute-done.23.refs_3_
  129.5 1.2 collective-permute-start.25
  130.7 2.0 %collective-permute-start.26 = (bf16[4,32,1152]{2,1,0:T(8,128)(2,1)}, bf16[4,32,1152]{2,1,0:T(8,128)(2,1)S(1)}, u32[]{:S(2)}, u32[]{:S(2)}) collective-permute-start(bf16[4,32,1152]{2,1,0:T(8,128)(2,1)} %get-tuple-element.87), channel_id=1, source_target_pairs={{0,24},{4,28},{8,16},{12,20},{16,8},{20,12},{24,0},{28,4},{1,25},{... | collective-permute-start | bytes 884744 | tf_op jit(solution)/shard_map/ppermute | solution.py:334
  132.7 0.1 collective-permute-start.27
  132.9 2.0 %collective-permute-start.19 = (bf16[4,32,1152]{2,1,0:T(8,128)(2,1)}, bf16[4,32,1152]{2,1,0:T(8,128)(2,1)S(1)}, u32[]{:S(2)}, u32[]{:S(2)}) collective-permute-start(bf16[4,32,1152]{2,1,0:T(8,128)(2,1)} %get-tuple-element.79), channel_id=1, source_target_pairs={{0,24},{4,28},{8,16},{12,20},{16,8},{20,12},{24,0},{28,4},{1,25},{... | collective-permute-start | bytes 884744 | tf_op jit(solution)/shard_map/ppermute | solution.py:334
  134.9 1.2 collective-permute-start.20
  136.1 1.7 shard_map.112.refs_0_
  137.8 25.6 %collective-permute-done.25.refs_5_ = bf16[4,32,1152]{2,1,0:T(8,128)(2,1)S(1)} collective-permute-done((bf16[4,32,1152]{2,1,0:T(8,128)(2,1)}, bf16[4,32,1152]{2,1,0:T(8,128)(2,1)S(1)}, u32[]{:S(2)}, u32[]{:S(2)}) %collective-permute-start.25) | collective-permute-done | bytes 294944 | tf_op jit(solution)/shard_map/ppermute | solution.py:334
  163.4 3.6 %collective-permute-start.37 = (bf16[40,1152]{1,0:T(8,128)(2,1)}, bf16[40,1152]{1,0:T(8,128)(2,1)S(1)}, u32[]{:S(2)}, u32[]{:S(2)}) collective-permute-start(bf16[40,1152]{1,0:T(8,128)(2,1)} %shard_map.112.refs_0_), channel_id=1, source_target_pairs={{0,3},{1,2},{2,1},{3,0},{4,7},{5,6},{6,5},{7,4},{8,11},{9,10},{10,... | collective-permute-start | bytes 276488 | tf_op jit(solution)/shard_map/ppermute | solution.py:334
  167.1 0.8 collective-permute-start.35
  167.9 2.7 %unpack.2 = (bf16[2,1,256,1152]{3,2,1,0:T(8,128)(2,1)}, bf16[2,1,256,1152]{3,2,1,0:T(8,128)(2,1)}, bf16[2,1,256,1152]{3,2,1,0:T(8,128)(2,1)}, bf16[2,1,256,1152]{3,2,1,0:T(8,128)(2,1)}) custom-call(bf16[4,32,1152]{2,1,0:T(8,128)(2,1)} %get-tuple-element.81.refs_0_, bf16[4,32,1152]{2,1,0:T(8,128)(2,1)} %copy-done.5, bf16[4,32,1152]{2,1,0:T(8,128)(2,1)} %copy-done.6, ...), custom_call_target="tpu_custom_call" | custom-call | tf_op jit(solution)/shard_map/unpack/pallas_call | solution.py:93
  170.6 0.7 copy-done.10
  171.4 2.7 %unpack.3 = (bf16[2,1,256,1152]{3,2,1,0:T(8,128)(2,1)}, bf16[2,1,256,1152]{3,2,1,0:T(8,128)(2,1)}, bf16[2,1,256,1152]{3,2,1,0:T(8,128)(2,1)}, bf16[2,1,256,1152]{3,2,1,0:T(8,128)(2,1)}) custom-call(bf16[4,32,1152]{2,1,0:T(8,128)(2,1)} %get-tuple-element.73.refs_0_, ...), custom_call_target="tpu_custom_call", output_to_operand_aliasing={{0}: (8, {}), {1}: (9, {}), {2}: (10, {}), {3}: (11, {})} | custom-call | tf_op jit(solution)/shard_map/unpack/pallas_call | solution.py:93
  174.2 1.6 collective-permute-done.36.refs_2_
  175.8 0.6 copy-done.35
  176.4 0.6 copy-done.37
  177.1 2.0 %shard_map.113 = f32[144,1152]{1,0:T(8,128)} custom-call(bf16[40,1152]{1,0:T(8,128)(2,1)} %shard_map.112.refs_0_, bf16[40,1152]{1,0:T(8,128)(2,1)} %copy-done.37, bf16[40,1152]{1,0:T(8,128)(2,1)} %copy-done.35, bf16[40,1152]{1,0:T(8,128)(2,1)} %copy-done.34), custom_call_target="tpu_custom_call" | custom-call | flops 1000000000 | bytes 4000000 | tf_op jit(solution)/shard_map/pallas_call | solution.py:280
  (104 shorter events, 0.9 us)
Async XLA Ops:
  2.6 12.1 %collective-permute-start.5 = (bf16[4,32,1152]{2,1,0:T(8,128)(2,1)}, bf16[4,32,1152]{2,1,0:T(8,128)(2,1)S(1)}, u32[]{:S(2)}, u32[]{:S(2)}) collective-permute-start(bf16[4,32,1152]{2,1,0:T(8,128)(2,1)} %get-tuple-element.62), channel_id=1, source_target_pairs={{0,24},{4,28},{8,16},{12,20},{16,8},{20,12},{24,0},{28,4},{1,25},{... | collective-permute-start | bytes 884744 | tf_op jit(solution)/shard_map/ppermute | solution.py:334
  6.6 14.0 %collective-permute-start.6 = (bf16[4,32,1152]{2,1,0:T(8,128)(2,1)}, bf16[4,32,1152]{2,1,0:T(8,128)(2,1)S(1)}, u32[]{:S(2)}, u32[]{:S(2)}) collective-permute-start(bf16[4,32,1152]{2,1,0:T(8,128)(2,1)} %get-tuple-element.63), channel_id=1, source_target_pairs={{0,28},{4,24},{8,20},{12,16},{16,12},{20,8},{24,4},{28,0},{1,29},{... | collective-permute-start | bytes 884744 | tf_op jit(solution)/shard_map/ppermute | solution.py:334
  8.5 18.8 %collective-permute-start.12 = (bf16[4,32,1152]{2,1,0:T(8,128)(2,1)}, bf16[4,32,1152]{2,1,0:T(8,128)(2,1)S(1)}, u32[]{:S(2)}, u32[]{:S(2)}) collective-permute-start(bf16[4,32,1152]{2,1,0:T(8,128)(2,1)} %get-tuple-element.70), channel_id=1, source_target_pairs={{0,24},{4,28},{8,16},{12,20},{16,8},{20,12},{24,0},{28,4},{1,25},{... | collective-permute-start | bytes 884744 | tf_op jit(solution)/shard_map/ppermute | solution.py:334
  10.7 22.6 %collective-permute-start.13 = (bf16[4,32,1152]{2,1,0:T(8,128)(2,1)}, bf16[4,32,1152]{2,1,0:T(8,128)(2,1)S(1)}, u32[]{:S(2)}, u32[]{:S(2)}) collective-permute-start(bf16[4,32,1152]{2,1,0:T(8,128)(2,1)} %get-tuple-element.71), channel_id=1, source_target_pairs={{0,28},{4,24},{8,20},{12,16},{16,12},{20,8},{24,4},{28,0},{1,29},{... | collective-permute-start | bytes 884744 | tf_op jit(solution)/shard_map/ppermute | solution.py:334
  13.8 23.8 %collective-permute-start.7 = (bf16[4,32,1152]{2,1,0:T(8,128)(2,1)}, bf16[4,32,1152]{2,1,0:T(8,128)(2,1)S(1)}, u32[]{:S(2)}, u32[]{:S(2)}) collective-permute-start(bf16[4,32,1152]{2,1,0:T(8,128)(2,1)} %get-tuple-element.65), channel_id=1, source_target_pairs={{0,4},{4,0},{8,12},{12,8},{16,20},{20,16},{24,28},{28,24},{1,5},{5... | collective-permute-start | bytes 884744 | tf_op jit(solution)/shard_map/ppermute | solution.py:334
  14.6 23.0 %copy-start.19 = (bf16[4,32,1152]{2,1,0:T(8,128)(2,1)}, bf16[4,32,1152]{2,1,0:T(8,128)(2,1)S(1)}, u32[]{:S(2)}) copy-start(bf16[4,32,1152]{2,1,0:T(8,128)(2,1)S(1)} %collective-permute-done.5.refs_6_) | copy-start | bytes 884740
  14.6 25.9 %collective-permute-start.8 = (bf16[4,32,1152]{2,1,0:T(8,128)(2,1)}, bf16[4,32,1152]{2,1,0:T(8,128)(2,1)S(1)}, u32[]{:S(2)}, u32[]{:S(2)}) collective-permute-start(bf16[4,32,1152]{2,1,0:T(8,128)(2,1)} %get-tuple-element.66), channel_id=1, source_target_pairs={{0,8},{4,12},{8,0},{12,4},{16,24},{20,28},{24,16},{28,20},{1,9},{5... | collective-permute-start | bytes 884744 | tf_op jit(solution)/shard_map/ppermute | solution.py:334
  20.6 17.0 %copy-start.20 = (bf16[4,32,1152]{2,1,0:T(8,128)(2,1)}, bf16[4,32,1152]{2,1,0:T(8,128)(2,1)S(1)}, u32[]{:S(2)}) copy-start(bf16[4,32,1152]{2,1,0:T(8,128)(2,1)S(1)} %collective-permute-done.6.refs_7_) | copy-start | bytes 884740
  20.6 25.3 %collective-permute-start.9 = (bf16[4,32,1152]{2,1,0:T(8,128)(2,1)}, bf16[4,32,1152]{2,1,0:T(8,128)(2,1)S(1)}, u32[]{:S(2)}, u32[]{:S(2)}) collective-permute-start(bf16[4,32,1152]{2,1,0:T(8,128)(2,1)} %get-tuple-element.67), channel_id=1, source_target_pairs={{0,12},{4,8},{8,4},{12,0},{16,28},{20,24},{24,20},{28,16},{1,13},{... | collective-permute-start | bytes 884744 | tf_op jit(solution)/shard_map/ppermute | solution.py:334
  27.3 10.3 %copy-start.21 = (bf16[4,32,1152]{2,1,0:T(8,128)(2,1)}, bf16[4,32,1152]{2,1,0:T(8,128)(2,1)S(1)}, u32[]{:S(2)}) copy-start(bf16[4,32,1152]{2,1,0:T(8,128)(2,1)S(1)} %collective-permute-done.12.refs_6_) | copy-start | bytes 884740
  27.3 20.5 %collective-permute-start.10 = (bf16[4,32,1152]{2,1,0:T(8,128)(2,1)}, bf16[4,32,1152]{2,1,0:T(8,128)(2,1)S(1)}, u32[]{:S(2)}, u32[]{:S(2)}) collective-permute-start(bf16[4,32,1152]{2,1,0:T(8,128)(2,1)} %get-tuple-element.68), channel_id=1, source_target_pairs={{0,16},{4,20},{8,24},{12,28},{16,0},{20,4},{24,8},{28,12},{1,17},{... | collective-permute-start | bytes 884744 | tf_op jit(solution)/shard_map/ppermute | solution.py:334
  33.3 4.3 %copy-start.22 = (bf16[4,32,1152]{2,1,0:T(8,128)(2,1)}, bf16[4,32,1152]{2,1,0:T(8,128)(2,1)S(1)}, u32[]{:S(2)}) copy-start(bf16[4,32,1152]{2,1,0:T(8,128)(2,1)S(1)} %collective-permute-done.13.refs_7_) | copy-start | bytes 884740
  33.3 15.0 %collective-permute-start.11 = (bf16[4,32,1152]{2,1,0:T(8,128)(2,1)}, bf16[4,32,1152]{2,1,0:T(8,128)(2,1)S(1)}, u32[]{:S(2)}, u32[]{:S(2)}) collective-permute-start(bf16[4,32,1152]{2,1,0:T(8,128)(2,1)} %get-tuple-element.69), channel_id=1, source_target_pairs={{0,20},{4,16},{8,28},{12,24},{16,4},{20,0},{24,12},{28,8},{1,21},{... | collective-permute-start | bytes 884744 | tf_op jit(solution)/shard_map/ppermute | solution.py:334
  37.7 10.6 %copy-start.23 = (bf16[4,32,1152]{2,1,0:T(8,128)(2,1)}, bf16[4,32,1152]{2,1,0:T(8,128)(2,1)S(1)}, u32[]{:S(2)}) copy-start(bf16[4,32,1152]{2,1,0:T(8,128)(2,1)S(1)} %collective-permute-done.7.refs_1_) | copy-start | bytes 884740
  37.7 25.9 %collective-permute-start = (bf16[4,32,1152]{2,1,0:T(8,128)(2,1)}, bf16[4,32,1152]{2,1,0:T(8,128)(2,1)S(1)}, u32[]{:S(2)}, u32[]{:S(2)}) collective-permute-start(bf16[4,32,1152]{2,1,0:T(8,128)(2,1)} %get-tuple-element.57), channel_id=1, source_target_pairs={{0,4},{4,0},{8,12},{12,8},{16,20},{20,16},{24,28},{28,24},{1,5},{5... | collective-permute-start | bytes 884744 | tf_op jit(solution)/shard_map/ppermute | solution.py:334
  40.5 7.8 %copy-start.24 = (bf16[4,32,1152]{2,1,0:T(8,128)(2,1)}, bf16[4,32,1152]{2,1,0:T(8,128)(2,1)S(1)}, u32[]{:S(2)}) copy-start(bf16[4,32,1152]{2,1,0:T(8,128)(2,1)S(1)} %collective-permute-done.8.refs_2_) | copy-start | bytes 884740
  40.5 23.1 %collective-permute-start.1 = (bf16[4,32,1152]{2,1,0:T(8,128)(2,1)}, bf16[4,32,1152]{2,1,0:T(8,128)(2,1)S(1)}, u32[]{:S(2)}, u32[]{:S(2)}) collective-permute-start(bf16[4,32,1152]{2,1,0:T(8,128)(2,1)} %get-tuple-element.58), channel_id=1, source_target_pairs={{0,8},{4,12},{8,0},{12,4},{16,24},{20,28},{24,16},{28,20},{1,9},{5... | collective-permute-start | bytes 884744 | tf_op jit(solution)/shard_map/ppermute | solution.py:334
  45.9 2.3 %copy-start.26 = (bf16[4,32,1152]{2,1,0:T(8,128)(2,1)}, bf16[4,32,1152]{2,1,0:T(8,128)(2,1)S(1)}, u32[]{:S(2)}) copy-start(bf16[4,32,1152]{2,1,0:T(8,128)(2,1)S(1)} %collective-permute-done.9.refs_3_) | copy-start | bytes 884740
  45.9 17.7 %collective-permute-start.2 = (bf16[4,32,1152]{2,1,0:T(8,128)(2,1)}, bf16[4,32,1152]{2,1,0:T(8,128)(2,1)S(1)}, u32[]{:S(2)}, u32[]{:S(2)}) collective-permute-start(bf16[4,32,1152]{2,1,0:T(8,128)(2,1)} %get-tuple-element.59), channel_id=1, source_target_pairs={{0,12},{4,8},{8,4},{12,0},{16,28},{20,24},{24,20},{28,16},{1,13},{... | collective-permute-start | bytes 884744 | tf_op jit(solution)/shard_map/ppermute | solution.py:334
  47.7 15.9 %collective-permute-start.3 = (bf16[4,32,1152]{2,1,0:T(8,128)(2,1)}, bf16[4,32,1152]{2,1,0:T(8,128)(2,1)S(1)}, u32[]{:S(2)}, u32[]{:S(2)}) collective-permute-start(bf16[4,32,1152]{2,1,0:T(8,128)(2,1)} %get-tuple-element.60), channel_id=1, source_target_pairs={{0,16},{4,20},{8,24},{12,28},{16,0},{20,4},{24,8},{28,12},{1,17},{... | collective-permute-start | bytes 884744 | tf_op jit(solution)/shard_map/ppermute | solution.py:334
  48.3 15.4 %collective-permute-start.4 = (bf16[4,32,1152]{2,1,0:T(8,128)(2,1)}, bf16[4,32,1152]{2,1,0:T(8,128)(2,1)S(1)}, u32[]{:S(2)}, u32[]{:S(2)}) collective-permute-start(bf16[4,32,1152]{2,1,0:T(8,128)(2,1)} %get-tuple-element.61), channel_id=1, source_target_pairs={{0,20},{4,16},{8,28},{12,24},{16,4},{20,0},{24,12},{28,8},{1,21},{... | collective-permute-start | bytes 884744 | tf_op jit(solution)/shard_map/ppermute | solution.py:334
  81.1 3.9 %collective-permute-start.28 = (bf16[4,144,1152]{2,1,0:T(8,128)(2,1)}, bf16[4,144,1152]{2,1,0:T(8,128)(2,1)S(1)}, u32[]{:S(2)}, u32[]{:S(2)}) collective-permute-start(bf16[4,144,1152]{2,1,0:T(8,128)(2,1)} %get-tuple-element.98), channel_id=1, source_target_pairs={{0,4},{4,0},{8,12},{12,8},{16,20},{20,16},{24,28},{28,24},{1,5},{5... | collective-permute-start | bytes 3981320 | tf_op jit(solution)/shard_map/ppermute | solution.py:334
  82.2 8.5 %collective-permute-start.14 = (bf16[4,32,1152]{2,1,0:T(8,128)(2,1)}, bf16[4,32,1152]{2,1,0:T(8,128)(2,1)S(1)}, u32[]{:S(2)}, u32[]{:S(2)}) collective-permute-start(bf16[4,32,1152]{2,1,0:T(8,128)(2,1)} %get-tuple-element.74), channel_id=1, source_target_pairs={{0,4},{4,0},{8,12},{12,8},{16,20},{20,16},{24,28},{28,24},{1,5},{5... | collective-permute-start | bytes 884744 | tf_op jit(solution)/shard_map/ppermute | solution.py:334
  82.2 10.5 %collective-permute-start.15 = (bf16[4,32,1152]{2,1,0:T(8,128)(2,1)}, bf16[4,32,1152]{2,1,0:T(8,128)(2,1)S(1)}, u32[]{:S(2)}, u32[]{:S(2)}) collective-permute-start(bf16[4,32,1152]{2,1,0:T(8,128)(2,1)} %get-tuple-element.75), channel_id=1, source_target_pairs={{0,8},{4,12},{8,0},{12,4},{16,24},{20,28},{24,16},{28,20},{1,9},{5... | collective-permute-start | bytes 884744 | tf_op jit(solution)/shard_map/ppermute | solution.py:334
  82.8 14.8 %collective-permute-start.16 = (bf16[4,32,1152]{2,1,0:T(8,128)(2,1)}, bf16[4,32,1152]{2,1,0:T(8,128)(2,1)S(1)}, u32[]{:S(2)}, u32[]{:S(2)}) collective-permute-start(bf16[4,32,1152]{2,1,0:T(8,128)(2,1)} %get-tuple-element.76), channel_id=1, source_target_pairs={{0,12},{4,8},{8,4},{12,0},{16,28},{20,24},{24,20},{28,16},{1,13},{... | collective-permute-start | bytes 884744 | tf_op jit(solution)/shard_map/ppermute | solution.py:334
  85.1 1.1 copy-start.14
  86.1 6.6 %copy-start.28 = (bf16[4,32,1152]{2,1,0:T(8,128)(2,1)S(1)}, bf16[4,32,1152]{2,1,0:T(8,128)(2,1)}, u32[]{:S(2)}) copy-start(bf16[4,32,1152]{2,1,0:T(8,128)(2,1)} %get-tuple-element.77) | copy-start | bytes 884740
  89.2 24.8 %collective-permute-start.29 = (bf16[144,1152]{1,0:T(8,128)(2,1)}, bf16[144,1152]{1,0:T(8,128)(2,1)S(1)}, u32[]{:S(2)}, u32[]{:S(2)}) collective-permute-start(bf16[144,1152]{1,0:T(8,128)(2,1)} %get-tuple-element.100), channel_id=1, source_target_pairs={{0,8},{4,12},{8,0},{12,4},{16,24},{20,28},{24,16},{28,20},{1,9},{5... | collective-permute-start | bytes 995336 | tf_op jit(solution)/shard_map/ppermute | solution.py:334
  89.7 25.9 %collective-permute-start.30 = (bf16[144,1152]{1,0:T(8,128)(2,1)}, bf16[144,1152]{1,0:T(8,128)(2,1)S(1)}, u32[]{:S(2)}, u32[]{:S(2)}) collective-permute-start(bf16[144,1152]{1,0:T(8,128)(2,1)} %get-tuple-element.101), channel_id=1, source_target_pairs={{0,16},{4,20},{8,24},{12,28},{16,0},{20,4},{24,8},{28,12},{1,17},{... | collective-permute-start | bytes 995336 | tf_op jit(solution)/shard_map/ppermute | solution.py:334
  90.7 28.6 %copy-start = (bf16[4,32,1152]{2,1,0:T(8,128)(2,1)}, bf16[4,32,1152]{2,1,0:T(8,128)(2,1)S(1)}, u32[]{:S(2)}) copy-start(bf16[4,32,1152]{2,1,0:T(8,128)(2,1)S(1)} %collective-permute-done.14.refs_1_) | copy-start | bytes 884740
  90.7 25.2 %collective-permute-start.31 = (bf16[144,1152]{1,0:T(8,128)(2,1)}, bf16[144,1152]{1,0:T(8,128)(2,1)S(1)}, u32[]{:S(2)}, u32[]{:S(2)}) collective-permute-start(bf16[144,1152]{1,0:T(8,128)(2,1)} %get-tuple-element.102), channel_id=1, source_target_pairs={{0,24},{4,28},{8,16},{12,20},{16,8},{20,12},{24,0},{28,4},{1,25},{... | collective-permute-start | bytes 995336 | tf_op jit(solution)/shard_map/ppermute | solution.py:334
  92.7 26.6 %copy-start.1 = (bf16[4,32,1152]{2,1,0:T(8,128)(2,1)}, bf16[4,32,1152]{2,1,0:T(8,128)(2,1)S(1)}, u32[]{:S(2)}) copy-start(bf16[4,32,1152]{2,1,0:T(8,128)(2,1)S(1)} %collective-permute-done.15.refs_2_) | copy-start | bytes 884740
  92.7 21.3 %collective-permute-start.17 = (bf16[4,32,1152]{2,1,0:T(8,128)(2,1)S(1)}, bf16[4,32,1152]{2,1,0:T(8,128)(2,1)S(1)}, u32[]{:S(2)}, u32[]{:S(2)}) collective-permute-start(bf16[4,32,1152]{2,1,0:T(8,128)(2,1)S(1)} %copy-done.28), channel_id=1, source_target_pairs={{0,16},{4,20},{8,24},{12,28},{16,0},{20,4},{24,8},{28,12},{1,17},{... | collective-permute-start | bytes 884744 | tf_op jit(solution)/shard_map/ppermute | solution.py:334
  97.6 21.7 %copy-start.2 = (bf16[4,32,1152]{2,1,0:T(8,128)(2,1)}, bf16[4,32,1152]{2,1,0:T(8,128)(2,1)S(1)}, u32[]{:S(2)}) copy-start(bf16[4,32,1152]{2,1,0:T(8,128)(2,1)S(1)} %collective-permute-done.16.refs_3_) | copy-start | bytes 884740
  97.6 21.7 %collective-permute-start.18 = (bf16[4,32,1152]{2,1,0:T(8,128)(2,1)}, bf16[4,32,1152]{2,1,0:T(8,128)(2,1)S(1)}, u32[]{:S(2)}, u32[]{:S(2)}) collective-permute-start(bf16[4,32,1152]{2,1,0:T(8,128)(2,1)} %get-tuple-element.78), channel_id=1, source_target_pairs={{0,20},{4,16},{8,28},{12,24},{16,4},{20,0},{24,12},{28,8},{1,21},{... | collective-permute-start | bytes 884744 | tf_op jit(solution)/shard_map/ppermute | solution.py:334
  114.0 5.3 %copy-start.3 = (bf16[4,32,1152]{2,1,0:T(8,128)(2,1)}, bf16[4,32,1152]{2,1,0:T(8,128)(2,1)S(1)}, u32[]{:S(2)}) copy-start(bf16[4,32,1152]{2,1,0:T(8,128)(2,1)S(1)} %collective-permute-done.17.refs_4_) | copy-start | bytes 884740
  114.0 6.9 %collective-permute-start.21 = (bf16[4,32,1152]{2,1,0:T(8,128)(2,1)}, bf16[4,32,1152]{2,1,0:T(8,128)(2,1)S(1)}, u32[]{:S(2)}, u32[]{:S(2)}) collective-permute-start(bf16[4,32,1152]{2,1,0:T(8,128)(2,1)} %get-tuple-element.82), channel_id=1, source_target_pairs={{0,4},{4,0},{8,12},{12,8},{16,20},{20,16},{24,28},{28,24},{1,5},{5... | collective-permute-start | bytes 884744 | tf_op jit(solution)/shard_map/ppermute | solution.py:334
  114.1 2.8 %copy-start.15 = (bf16[144,1152]{1,0:T(8,128)(2,1)}, bf16[144,1152]{1,0:T(8,128)(2,1)S(1)}, u32[]{:S(2)}) copy-start(bf16[144,1152]{1,0:T(8,128)(2,1)S(1)} %collective-permute-done.29.refs_0_) | copy-start | bytes 995332
  114.1 10.2 %collective-permute-start.22 = (bf16[4,32,1152]{2,1,0:T(8,128)(2,1)}, bf16[4,32,1152]{2,1,0:T(8,128)(2,1)S(1)}, u32[]{:S(2)}, u32[]{:S(2)}) collective-permute-start(bf16[4,32,1152]{2,1,0:T(8,128)(2,1)} %get-tuple-element.83), channel_id=1, source_target_pairs={{0,8},{4,12},{8,0},{12,4},{16,24},{20,28},{24,16},{28,20},{1,9},{5... | collective-permute-start | bytes 884744 | tf_op jit(solution)/shard_map/ppermute | solution.py:334
  115.6 1.2 copy-start.16
  115.6 13.8 %collective-permute-start.23 = (bf16[4,32,1152]{2,1,0:T(8,128)(2,1)}, bf16[4,32,1152]{2,1,0:T(8,128)(2,1)S(1)}, u32[]{:S(2)}, u32[]{:S(2)}) collective-permute-start(bf16[4,32,1152]{2,1,0:T(8,128)(2,1)} %get-tuple-element.84), channel_id=1, source_target_pairs={{0,12},{4,8},{8,4},{12,0},{16,28},{20,24},{24,20},{28,16},{1,13},{... | collective-permute-start | bytes 884744 | tf_op jit(solution)/shard_map/ppermute | solution.py:334
  115.9 14.7 %collective-permute-start.24 = (bf16[4,32,1152]{2,1,0:T(8,128)(2,1)}, bf16[4,32,1152]{2,1,0:T(8,128)(2,1)S(1)}, u32[]{:S(2)}, u32[]{:S(2)}) collective-permute-start(bf16[4,32,1152]{2,1,0:T(8,128)(2,1)} %get-tuple-element.85), channel_id=1, source_target_pairs={{0,16},{4,20},{8,24},{12,28},{16,0},{20,4},{24,8},{28,12},{1,17},{... | collective-permute-start | bytes 884744 | tf_op jit(solution)/shard_map/ppermute | solution.py:334
  116.9 15.8 %copy-start.18 = (bf16[4,32,1152]{2,1,0:T(8,128)(2,1)S(1)}, bf16[4,32,1152]{2,1,0:T(8,128)(2,1)}, u32[]{:S(2)}) copy-start(bf16[4,32,1152]{2,1,0:T(8,128)(2,1)} %get-tuple-element.88) | copy-start | bytes 884740
  119.3 18.5 %copy-start.4 = (bf16[4,32,1152]{2,1,0:T(8,128)(2,1)}, bf16[4,32,1152]{2,1,0:T(8,128)(2,1)S(1)}, u32[]{:S(2)}) copy-start(bf16[4,32,1152]{2,1,0:T(8,128)(2,1)S(1)} %collective-permute-done.18.refs_5_) | copy-start | bytes 884740
  119.3 13.4 %collective-permute-start.32 = (bf16[40,1152]{1,0:T(8,128)(2,1)}, bf16[40,1152]{1,0:T(8,128)(2,1)S(1)}, u32[]{:S(2)}, u32[]{:S(2)}) collective-permute-start(bf16[40,1152]{1,0:T(8,128)(2,1)} %get-tuple-element.104), channel_id=1, source_target_pairs={{0,1},{1,0},{2,3},{3,2},{4,5},{5,4},{6,7},{7,6},{8,9},{9,8},{10,11... | collective-permute-start | bytes 276488 | tf_op jit(solution)/shard_map/ppermute | solution.py:334
  121.0 16.8 %copy-start.5 = (bf16[4,32,1152]{2,1,0:T(8,128)(2,1)}, bf16[4,32,1152]{2,1,0:T(8,128)(2,1)S(1)}, u32[]{:S(2)}) copy-start(bf16[4,32,1152]{2,1,0:T(8,128)(2,1)S(1)} %collective-permute-done.21.refs_1_) | copy-start | bytes 884740
  121.0 11.9 %collective-permute-start.33 = (bf16[40,1152]{1,0:T(8,128)(2,1)}, bf16[40,1152]{1,0:T(8,128)(2,1)S(1)}, u32[]{:S(2)}, u32[]{:S(2)}) collective-permute-start(bf16[40,1152]{1,0:T(8,128)(2,1)} %get-tuple-element.105), channel_id=1, source_target_pairs={{0,2},{1,3},{2,0},{3,1},{4,6},{5,7},{6,4},{7,5},{8,10},{9,11},{10,... | collective-permute-start | bytes 276488 | tf_op jit(solution)/shard_map/ppermute | solution.py:334
  124.2 13.6 %copy-start.6 = (bf16[4,32,1152]{2,1,0:T(8,128)(2,1)}, bf16[4,32,1152]{2,1,0:T(8,128)(2,1)S(1)}, u32[]{:S(2)}) copy-start(bf16[4,32,1152]{2,1,0:T(8,128)(2,1)S(1)} %collective-permute-done.22.refs_2_) | copy-start | bytes 884740
  124.2 10.6 %collective-permute-start.34 = (bf16[40,1152]{1,0:T(8,128)(2,1)}, bf16[40,1152]{1,0:T(8,128)(2,1)S(1)}, u32[]{:S(2)}, u32[]{:S(2)}) collective-permute-start(bf16[40,1152]{1,0:T(8,128)(2,1)} %get-tuple-element.106), channel_id=1, source_target_pairs={{0,3},{1,2},{2,1},{3,0},{4,7},{5,6},{6,5},{7,4},{8,11},{9,10},{10,... | collective-permute-start | bytes 276488 | tf_op jit(solution)/shard_map/ppermute | solution.py:334
  129.5 8.3 %copy-start.7 = (bf16[4,32,1152]{2,1,0:T(8,128)(2,1)}, bf16[4,32,1152]{2,1,0:T(8,128)(2,1)S(1)}, u32[]{:S(2)}) copy-start(bf16[4,32,1152]{2,1,0:T(8,128)(2,1)S(1)} %collective-permute-done.23.refs_3_) | copy-start | bytes 884740
  129.5 34.0 %collective-permute-start.25 = (bf16[4,32,1152]{2,1,0:T(8,128)(2,1)}, bf16[4,32,1152]{2,1,0:T(8,128)(2,1)S(1)}, u32[]{:S(2)}, u32[]{:S(2)}) collective-permute-start(bf16[4,32,1152]{2,1,0:T(8,128)(2,1)} %get-tuple-element.86), channel_id=1, source_target_pairs={{0,20},{4,16},{8,28},{12,24},{16,4},{20,0},{24,12},{28,8},{1,21},{... | collective-permute-start | bytes 884744 | tf_op jit(solution)/shard_map/ppermute | solution.py:334
  130.7 7.1 %copy-start.8 = (bf16[4,32,1152]{2,1,0:T(8,128)(2,1)}, bf16[4,32,1152]{2,1,0:T(8,128)(2,1)S(1)}, u32[]{:S(2)}) copy-start(bf16[4,32,1152]{2,1,0:T(8,128)(2,1)S(1)} %collective-permute-done.24.refs_4_) | copy-start | bytes 884740
  130.7 36.4 %collective-permute-start.26 = (bf16[4,32,1152]{2,1,0:T(8,128)(2,1)}, bf16[4,32,1152]{2,1,0:T(8,128)(2,1)S(1)}, u32[]{:S(2)}, u32[]{:S(2)}) collective-permute-start(bf16[4,32,1152]{2,1,0:T(8,128)(2,1)} %get-tuple-element.87), channel_id=1, source_target_pairs={{0,24},{4,28},{8,16},{12,20},{16,8},{20,12},{24,0},{28,4},{1,25},{... | collective-permute-start | bytes 884744 | tf_op jit(solution)/shard_map/ppermute | solution.py:334
  132.7 3.4 %copy-start.36 = (bf16[40,1152]{1,0:T(8,128)(2,1)}, bf16[40,1152]{1,0:T(8,128)(2,1)S(1)}, u32[]{:S(2)}) copy-start(bf16[40,1152]{1,0:T(8,128)(2,1)S(1)} %collective-permute-done.32.refs_0_) | copy-start | bytes 276484
  132.7 34.3 %collective-permute-start.27 = (bf16[4,32,1152]{2,1,0:T(8,128)(2,1)S(1)}, bf16[4,32,1152]{2,1,0:T(8,128)(2,1)S(1)}, u32[]{:S(2)}, u32[]{:S(2)}) collective-permute-start(bf16[4,32,1152]{2,1,0:T(8,128)(2,1)S(1)} %copy-done.18), channel_id=1, source_target_pairs={{0,28},{4,24},{8,20},{12,16},{16,12},{20,8},{24,4},{28,0},{1,29},{... | collective-permute-start | bytes 884744 | tf_op jit(solution)/shard_map/ppermute | solution.py:334
  132.9 3.2 %copy-start.38 = (bf16[40,1152]{1,0:T(8,128)(2,1)}, bf16[40,1152]{1,0:T(8,128)(2,1)S(1)}, u32[]{:S(2)}) copy-start(bf16[40,1152]{1,0:T(8,128)(2,1)S(1)} %collective-permute-done.33.refs_1_) | copy-start | bytes 276484
  132.9 37.7 %collective-permute-start.19 = (bf16[4,32,1152]{2,1,0:T(8,128)(2,1)}, bf16[4,32,1152]{2,1,0:T(8,128)(2,1)S(1)}, u32[]{:S(2)}, u32[]{:S(2)}) collective-permute-start(bf16[4,32,1152]{2,1,0:T(8,128)(2,1)} %get-tuple-element.79), channel_id=1, source_target_pairs={{0,24},{4,28},{8,16},{12,20},{16,8},{20,12},{24,0},{28,4},{1,25},{... | collective-permute-start | bytes 884744 | tf_op jit(solution)/shard_map/ppermute | solution.py:334
  134.9 1.2 copy-start.39
  134.9 35.7 %collective-permute-start.20 = (bf16[4,32,1152]{2,1,0:T(8,128)(2,1)}, bf16[4,32,1152]{2,1,0:T(8,128)(2,1)S(1)}, u32[]{:S(2)}, u32[]{:S(2)}) collective-permute-start(bf16[4,32,1152]{2,1,0:T(8,128)(2,1)} %get-tuple-element.80), channel_id=1, source_target_pairs={{0,28},{4,24},{8,20},{12,16},{16,12},{20,8},{24,4},{28,0},{1,29},{... | collective-permute-start | bytes 884744 | tf_op jit(solution)/shard_map/ppermute | solution.py:334
  163.4 4.4 %copy-start.9 = (bf16[4,32,1152]{2,1,0:T(8,128)(2,1)}, bf16[4,32,1152]{2,1,0:T(8,128)(2,1)S(1)}, u32[]{:S(2)}) copy-start(bf16[4,32,1152]{2,1,0:T(8,128)(2,1)S(1)} %collective-permute-done.25.refs_5_) | copy-start | bytes 884740
  163.4 10.7 %collective-permute-start.37 = (bf16[40,1152]{1,0:T(8,128)(2,1)}, bf16[40,1152]{1,0:T(8,128)(2,1)S(1)}, u32[]{:S(2)}, u32[]{:S(2)}) collective-permute-start(bf16[40,1152]{1,0:T(8,128)(2,1)} %shard_map.112.refs_0_), channel_id=1, source_target_pairs={{0,3},{1,2},{2,1},{3,0},{4,7},{5,6},{6,5},{7,4},{8,11},{9,10},{10,... | collective-permute-start | bytes 276488 | tf_op jit(solution)/shard_map/ppermute | solution.py:334
  167.0 8.8 %collective-permute-start.36 = (bf16[40,1152]{1,0:T(8,128)(2,1)}, bf16[40,1152]{1,0:T(8,128)(2,1)S(1)}, u32[]{:S(2)}, u32[]{:S(2)}) collective-permute-start(bf16[40,1152]{1,0:T(8,128)(2,1)} %shard_map.112.refs_0_), channel_id=1, source_target_pairs={{0,2},{1,3},{2,0},{3,1},{4,6},{5,7},{6,4},{7,5},{8,10},{9,11},{10,... | collective-permute-start | bytes 276488 | tf_op jit(solution)/shard_map/ppermute | solution.py:334
  167.1 8.7 %collective-permute-start.35 = (bf16[40,1152]{1,0:T(8,128)(2,1)}, bf16[40,1152]{1,0:T(8,128)(2,1)S(1)}, u32[]{:S(2)}, u32[]{:S(2)}) collective-permute-start(bf16[40,1152]{1,0:T(8,128)(2,1)} %shard_map.112.refs_0_), channel_id=1, source_target_pairs={{0,1},{1,0},{2,3},{3,2},{4,5},{5,4},{6,7},{7,6},{8,9},{9,8},{10,11... | collective-permute-start | bytes 276488 | tf_op jit(solution)/shard_map/ppermute | solution.py:334
  174.2 1.7 copy-start.34
  (14 other events, 11.1 us)
